TPU v7x, 32 devices: a whole 2x2x4 slice. The times are simulated.
32 devices in a mesh: data: 2 (over x), model: 4 (over z), stage: 4 (over y, core).
Axes of the slice: x: 2, y: 2, z: 4, core: 2. Of those that a mesh axis runs over, the one named last changes fastest.
Arguments:
- inputs: bfloat16 [12, 256, 2048], P('data'), parts along dimension 0
- targets: bfloat16 [12, 256, 2048], P('data'), parts along dimension 0
- w_in: bfloat16 [4, 1, 2048, 8192], P('stage', None, None, 'model')
- w_out: bfloat16 [4, 1, 8192, 2048], P('stage', None, 'model')
Outputs:
- output 1: float32 [8, 1, 2048, 8192], P(('data', 'stage'), None, None, 'model'), parts along dimension 0
- output 2: float32 [8, 1, 8192, 2048], P(('data', 'stage'), None, 'model'), parts along dimension 0
- output 3: float32 [2], P('data'), parts along dimension 0
There are 2 independent parts. A program takes and returns all parts, laid end to end along the dimension named above; an argument that names none is the same for every part.
All inputs are finite; a program needn't handle non-finite values.
Results may differ from a plain program's by a relative error of at most 0.00873894.
Values are sent between devices in bfloat16 or wider.
A program may use at most 1 GiB of HBM per device.

v0:
```python
import jax
import jax.numpy as jnp
from jax import lax
from jax.sharding import PartitionSpec as P

GELU_COEF = 0.7978845608028654
CUBIC_COEF = 0.044715


def gelu_tanh(values):
    inner_arg = GELU_COEF * (values + CUBIC_COEF * values * values * values)
    return 0.5 * values * (1.0 + jnp.tanh(inner_arg))


def gelu_slope(values):
    tanh_val = jnp.tanh(GELU_COEF * (values + CUBIC_COEF * values * values * values))
    return 0.5 * (1.0 + tanh_val) + 0.5 * values * (1.0 - tanh_val * tanh_val) * GELU_COEF * (1.0 + 3.0 * CUBIC_COEF * values * values)


def solution(mesh):
    n_stage = mesh.shape["stage"]
    down_perm = [(src_pos, src_pos + 1) for src_pos in range(n_stage - 1)]
    up_perm = [(src_pos + 1, src_pos) for src_pos in range(n_stage - 1)]

    def stage_step(inputs, targets, w_in, w_out):
        num_micro, num_tokens, model_dim = inputs.shape
        layers_here = w_in.shape[1]
        w_in_loc = w_in[0]
        w_out_loc = w_out[0]
        stage_pos = lax.axis_index("stage")
        is_last = stage_pos == n_stage - 1
        num_ticks = num_micro + n_stage - 1
        grad_scale = 1.0 / (num_micro * num_tokens * model_dim)

        def fwd_tick(state_in, tick_num):
            recv_act, loss_sum = state_in
            mb_index = tick_num - stage_pos
            first_in = lax.dynamic_index_in_dim(inputs, jnp.clip(tick_num, 0, num_micro - 1), 0, keepdims=False)
            hidden = jnp.where(stage_pos == 0, first_in, recv_act)
            saved_in = []
            saved_pre = []
            saved_act = []
            for layer_pos in range(layers_here):
                pre_act = jnp.dot(hidden, w_in_loc[layer_pos], preferred_element_type=jnp.float32).astype(jnp.bfloat16)
                act_out = gelu_tanh(pre_act.astype(jnp.float32)).astype(jnp.bfloat16)
                part_sum = jnp.dot(act_out, w_out_loc[layer_pos], preferred_element_type=jnp.float32)
                saved_in.append(hidden)
                saved_pre.append(pre_act)
                saved_act.append(act_out)
                hidden = (hidden.astype(jnp.float32) + lax.psum(part_sum, "model")).astype(jnp.bfloat16)
            tgt_mb = lax.dynamic_index_in_dim(targets, jnp.clip(mb_index, 0, num_micro - 1), 0, keepdims=False)
            out_err = hidden.astype(jnp.float32) - tgt_mb.astype(jnp.float32)
            start_grad = (out_err * grad_scale).astype(jnp.bfloat16)
            keep_loss = is_last & (mb_index >= 0) & (mb_index < num_micro)
            loss_sum = loss_sum + jnp.where(keep_loss, 0.5 * jnp.sum(out_err * out_err), 0.0)
            sent_act = lax.ppermute(hidden, "stage", down_perm)
            return (sent_act, loss_sum), (jnp.stack(saved_in), jnp.stack(saved_pre), jnp.stack(saved_act), start_grad)

        fwd_init = (jnp.zeros((num_tokens, model_dim), jnp.bfloat16), jnp.zeros((), jnp.float32))
        (last_act, loss_sum), (all_in, all_pre, all_act, all_start) = lax.scan(fwd_tick, fwd_init, jnp.arange(num_ticks))

        def bwd_tick(state_in, tick_num):
            recv_grad, acc_in, acc_out = state_in
            mb_index = tick_num - (n_stage - 1 - stage_pos)
            is_valid = (mb_index >= 0) & (mb_index < num_micro)
            save_pos = jnp.clip(mb_index + stage_pos, 0, num_ticks - 1)
            start_here = lax.dynamic_index_in_dim(all_start, save_pos, 0, keepdims=False)
            grad_h = jnp.where(is_last, start_here, recv_grad)
            grad_h = jnp.where(is_valid, grad_h, jnp.zeros_like(grad_h))
            layer_in = lax.dynamic_index_in_dim(all_in, save_pos, 0, keepdims=False)
            layer_pre = lax.dynamic_index_in_dim(all_pre, save_pos, 0, keepdims=False)
            layer_act = lax.dynamic_index_in_dim(all_act, save_pos, 0, keepdims=False)
            new_in = list(acc_in)
            new_out = list(acc_out)
            for layer_pos in reversed(range(layers_here)):
                grad_act = jnp.einsum("bd,fd->bf", grad_h, w_out_loc[layer_pos], preferred_element_type=jnp.float32).astype(jnp.bfloat16)
                grad_pre = (gelu_slope(layer_pre[layer_pos].astype(jnp.float32)) * grad_act.astype(jnp.float32)).astype(jnp.bfloat16)
                new_out[layer_pos] = new_out[layer_pos] + jnp.einsum("bf,bd->fd", layer_act[layer_pos], grad_h, preferred_element_type=jnp.float32)
                new_in[layer_pos] = new_in[layer_pos] + jnp.einsum("bd,bf->df", layer_in[layer_pos], grad_pre, preferred_element_type=jnp.float32)
                part_sum = jnp.einsum("bf,df->bd", grad_pre, w_in_loc[layer_pos], preferred_element_type=jnp.float32)
                grad_h = (grad_h.astype(jnp.float32) + lax.psum(part_sum, "model")).astype(jnp.bfloat16)
            sent_grad = lax.ppermute(grad_h, "stage", up_perm)
            return (sent_grad, tuple(new_in), tuple(new_out)), None

        zeros_in = tuple(jnp.zeros(w_in_loc.shape[1:], jnp.float32) for layer_pos in range(layers_here))
        zeros_out = tuple(jnp.zeros(w_out_loc.shape[1:], jnp.float32) for layer_pos in range(layers_here))
        bwd_init = (jnp.zeros((num_tokens, model_dim), jnp.bfloat16), zeros_in, zeros_out)
        (first_grad, acc_in, acc_out), unused_ys = lax.scan(bwd_tick, bwd_init, jnp.arange(num_ticks))
        loss_out = jnp.reshape(lax.psum(loss_sum, "stage") * grad_scale, (1,))
        return jnp.stack(acc_in)[None], jnp.stack(acc_out)[None], loss_out

    return jax.shard_map(
        stage_step,
        mesh=mesh,
        in_specs=(P("data", None, None), P("data", None, None), P("stage", None, None, "model"), P("stage", None, "model", None)),
        out_specs=(P(("data", "stage"), None, None, "model"), P(("data", "stage"), None, "model", None), P("data")),
        check_vma=False,
    )
```

profile of v0, /device:TPU:0, one launch (start us, length us, event | category | flops | bytes accessed | tf_op | source)
XLA Modules:
  0.0 2167.0 jit_solution(8587782935021615360)
XLA Ops:
  7.3 1077.1 %while.37 = (s32[]{:T(128)}, bf16[256,2048]{1,0:T(8,128)(2,1)S(1)}, f32[]{:T(128)}, bf16[9,1,256,2048]{3,2,1,0:T(8,128)(2,1)}, bf16[9,1,256,2048]{3,2,1,0:T(8,12...) while((s32[]{:T(128)}, bf16[256,2048]{1,0:T(8,128)(2,1)S(1)}, ...), condition=%wide.region_3.4_spmd, body=%wide.region_0.3_spmd.sunk | while | flops 4313841664 | bytes 78645712 | solution.py:60
  23.9 87.8 %all-reduce.3.cloned.1.call-done = f32[256,2048]{1,0:T(8,128)} async-done(((f32[256,2048]{1,0:T(8,128)}), f32[256,2048]{1,0:T(8,128)}) %all-reduce.3.cloned.1.call-update) | async-done | bytes 2097168 | tf_op jit(solution)/shard_map/while/body/eval_jaxpr/psum | solution.py:50
  136.2 96.1 %all-reduce.3.cloned.1.call-done = f32[256,2048]{1,0:T(8,128)} async-done(((f32[256,2048]{1,0:T(8,128)}), f32[256,2048]{1,0:T(8,128)}) %all-reduce.3.cloned.1.call-update) | async-done | bytes 2097168 | tf_op jit(solution)/shard_map/while/body/eval_jaxpr/psum | solution.py:50
  256.8 96.1 %all-reduce.3.cloned.1.call-done = f32[256,2048]{1,0:T(8,128)} async-done(((f32[256,2048]{1,0:T(8,128)}), f32[256,2048]{1,0:T(8,128)}) %all-reduce.3.cloned.1.call-update) | async-done | bytes 2097168 | tf_op jit(solution)/shard_map/while/body/eval_jaxpr/psum | solution.py:50
  377.4 96.1 %all-reduce.3.cloned.1.call-done = f32[256,2048]{1,0:T(8,128)} async-done(((f32[256,2048]{1,0:T(8,128)}), f32[256,2048]{1,0:T(8,128)}) %all-reduce.3.cloned.1.call-update) | async-done | bytes 2097168 | tf_op jit(solution)/shard_map/while/body/eval_jaxpr/psum | solution.py:50
  498.0 96.1 %all-reduce.3.cloned.1.call-done = f32[256,2048]{1,0:T(8,128)} async-done(((f32[256,2048]{1,0:T(8,128)}), f32[256,2048]{1,0:T(8,128)}) %all-reduce.3.cloned.1.call-update) | async-done | bytes 2097168 | tf_op jit(solution)/shard_map/while/body/eval_jaxpr/psum | solution.py:50
  618.6 96.1 %all-reduce.3.cloned.1.call-done = f32[256,2048]{1,0:T(8,128)} async-done(((f32[256,2048]{1,0:T(8,128)}), f32[256,2048]{1,0:T(8,128)}) %all-reduce.3.cloned.1.call-update) | async-done | bytes 2097168 | tf_op jit(solution)/shard_map/while/body/eval_jaxpr/psum | solution.py:50
  739.2 96.1 %all-reduce.3.cloned.1.call-done = f32[256,2048]{1,0:T(8,128)} async-done(((f32[256,2048]{1,0:T(8,128)}), f32[256,2048]{1,0:T(8,128)}) %all-reduce.3.cloned.1.call-update) | async-done | bytes 2097168 | tf_op jit(solution)/shard_map/while/body/eval_jaxpr/psum | solution.py:50
  859.8 96.1 %all-reduce.3.cloned.1.call-done = f32[256,2048]{1,0:T(8,128)} async-done(((f32[256,2048]{1,0:T(8,128)}), f32[256,2048]{1,0:T(8,128)}) %all-reduce.3.cloned.1.call-update) | async-done | bytes 2097168 | tf_op jit(solution)/shard_map/while/body/eval_jaxpr/psum | solution.py:50
  980.4 96.1 %all-reduce.3.cloned.1.call-done = f32[256,2048]{1,0:T(8,128)} async-done(((f32[256,2048]{1,0:T(8,128)}), f32[256,2048]{1,0:T(8,128)}) %all-reduce.3.cloned.1.call-update) | async-done | bytes 2097168 | tf_op jit(solution)/shard_map/while/body/eval_jaxpr/psum | solution.py:50
  1084.5 18.0 psum.23
  1103.3 1055.7 %while.38 = (s32[]{:T(128)}, bf16[256,2048]{1,0:T(8,128)(2,1)S(1)}, f32[2048,2048]{1,0:T(8,128)}, f32[2048,2048]{1,0:T(8,128)}, s32[9]{0:T(128)S(1)}, /*index=5*...) while((s32[]{:T(128)}, bf16[256,2048]{1,0:T(8,128)(2,1)S(1)}, ...), condition=%wide.region_6.7_spmd.clone, body=%wide.region_4.6_spmd.clone.sunk | while | flops 8621391872 | bytes 143655312 | solution.py:88
  1126.8 76.1 %all-reduce.5.cloned.1.call-done = f32[256,2048]{1,0:T(8,128)} async-done(((f32[256,2048]{1,0:T(8,128)}), f32[256,2048]{1,0:T(8,128)}) %all-reduce.5.cloned.1.call-update) | async-done | bytes 2097168 | tf_op jit(solution)/shard_map/while/body/eval_jaxpr/psum | solution.py:81
  1229.6 14.7 select_add_fusion.5
  1244.3 74.1 %all-reduce.5.cloned.1.call-done = f32[256,2048]{1,0:T(8,128)} async-done(((f32[256,2048]{1,0:T(8,128)}), f32[256,2048]{1,0:T(8,128)}) %all-reduce.5.cloned.1.call-update) | async-done | bytes 2097168 | tf_op jit(solution)/shard_map/while/body/eval_jaxpr/psum | solution.py:81
  1349.9 14.7 select_add_fusion.5
  1364.6 71.4 %all-reduce.5.cloned.1.call-done = f32[256,2048]{1,0:T(8,128)} async-done(((f32[256,2048]{1,0:T(8,128)}), f32[256,2048]{1,0:T(8,128)}) %all-reduce.5.cloned.1.call-update) | async-done | bytes 2097168 | tf_op jit(solution)/shard_map/while/body/eval_jaxpr/psum | solution.py:81
  1439.1 14.7 select_add_fusion.4
  1467.5 14.7 select_add_fusion.5
  1482.2 71.3 %all-reduce.5.cloned.1.call-done = f32[256,2048]{1,0:T(8,128)} async-done(((f32[256,2048]{1,0:T(8,128)}), f32[256,2048]{1,0:T(8,128)}) %all-reduce.5.cloned.1.call-update) | async-done | bytes 2097168 | tf_op jit(solution)/shard_map/while/body/eval_jaxpr/psum | solution.py:81
  1585.0 14.7 select_add_fusion.5
  1599.7 71.3 %all-reduce.5.cloned.1.call-done = f32[256,2048]{1,0:T(8,128)} async-done(((f32[256,2048]{1,0:T(8,128)}), f32[256,2048]{1,0:T(8,128)}) %all-reduce.5.cloned.1.call-update) | async-done | bytes 2097168 | tf_op jit(solution)/shard_map/while/body/eval_jaxpr/psum | solution.py:81
  1674.2 14.7 select_add_fusion.4
  1702.5 14.7 select_add_fusion.5
  1717.2 71.3 %all-reduce.5.cloned.1.call-done = f32[256,2048]{1,0:T(8,128)} async-done(((f32[256,2048]{1,0:T(8,128)}), f32[256,2048]{1,0:T(8,128)}) %all-reduce.5.cloned.1.call-update) | async-done | bytes 2097168 | tf_op jit(solution)/shard_map/while/body/eval_jaxpr/psum | solution.py:81
  1820.1 14.7 select_add_fusion.5
  1834.7 71.3 %all-reduce.5.cloned.1.call-done = f32[256,2048]{1,0:T(8,128)} async-done(((f32[256,2048]{1,0:T(8,128)}), f32[256,2048]{1,0:T(8,128)}) %all-reduce.5.cloned.1.call-update) | async-done | bytes 2097168 | tf_op jit(solution)/shard_map/while/body/eval_jaxpr/psum | solution.py:81
  1909.3 14.7 select_add_fusion.4
  1937.6 14.7 select_add_fusion.5
  1952.3 71.3 %all-reduce.5.cloned.1.call-done = f32[256,2048]{1,0:T(8,128)} async-done(((f32[256,2048]{1,0:T(8,128)}), f32[256,2048]{1,0:T(8,128)}) %all-reduce.5.cloned.1.call-update) | async-done | bytes 2097168 | tf_op jit(solution)/shard_map/while/body/eval_jaxpr/psum | solution.py:81
  2055.1 14.7 select_add_fusion.5
  2069.8 71.3 %all-reduce.5.cloned.1.call-done = f32[256,2048]{1,0:T(8,128)} async-done(((f32[256,2048]{1,0:T(8,128)}), f32[256,2048]{1,0:T(8,128)}) %all-reduce.5.cloned.1.call-update) | async-done | bytes 2097168 | tf_op jit(solution)/shard_map/while/body/eval_jaxpr/psum | solution.py:81
  (278 shorter events, 440.0 us)
Async XLA Ops:
  7.4 104.4 %all-reduce.3.cloned.1.call-start = ((), (), s32[]{:S(2)}) async-start(), calls=%async_computation | async-start | bytes 4194304 | tf_op jit(solution)/shard_map/while/body/eval_jaxpr/psum | solution.py:50
  115.2 4.4 collective-permute-start
  119.7 112.7 %all-reduce.3.cloned.1.call-start = ((), (), s32[]{:S(2)}) async-start(), calls=%async_computation | async-start | bytes 4194304 | tf_op jit(solution)/shard_map/while/body/eval_jaxpr/psum | solution.py:50
  235.9 4.4 collective-permute-start
  240.3 112.6 %all-reduce.3.cloned.1.call-start = ((), (), s32[]{:S(2)}) async-start(), calls=%async_computation | async-start | bytes 4194304 | tf_op jit(solution)/shard_map/while/body/eval_jaxpr/psum | solution.py:50
  356.4 4.4 collective-permute-start
  360.8 112.7 %all-reduce.3.cloned.1.call-start = ((), (), s32[]{:S(2)}) async-start(), calls=%async_computation | async-start | bytes 4194304 | tf_op jit(solution)/shard_map/while/body/eval_jaxpr/psum | solution.py:50
  481.4 112.6 %all-reduce.3.cloned.1.call-start = ((), (), s32[]{:S(2)}) async-start(), calls=%async_computation | async-start | bytes 4194304 | tf_op jit(solution)/shard_map/while/body/eval_jaxpr/psum | solution.py:50
  597.5 4.4 collective-permute-start
  602.0 112.7 %all-reduce.3.cloned.1.call-start = ((), (), s32[]{:S(2)}) async-start(), calls=%async_computation | async-start | bytes 4194304 | tf_op jit(solution)/shard_map/while/body/eval_jaxpr/psum | solution.py:50
  722.6 112.8 %all-reduce.3.cloned.1.call-start = ((), (), s32[]{:S(2)}) async-start(), calls=%async_computation | async-start | bytes 4194304 | tf_op jit(solution)/shard_map/while/body/eval_jaxpr/psum | solution.py:50
  838.8 4.4 collective-permute-start
  843.3 112.7 %all-reduce.3.cloned.1.call-start = ((), (), s32[]{:S(2)}) async-start(), calls=%async_computation | async-start | bytes 4194304 | tf_op jit(solution)/shard_map/while/body/eval_jaxpr/psum | solution.py:50
  963.8 112.7 %all-reduce.3.cloned.1.call-start = ((), (), s32[]{:S(2)}) async-start(), calls=%async_computation | async-start | bytes 4194304 | tf_op jit(solution)/shard_map/while/body/eval_jaxpr/psum | solution.py:50
  1103.3 99.7 %all-reduce.5.cloned.1.call-start = ((), (), s32[]{:S(2)}) async-start(), calls=%async_computation.1 | async-start | bytes 4194304 | tf_op jit(solution)/shard_map/while/body/eval_jaxpr/psum | solution.py:81
  1204.8 11.1 collective-permute-start.1
  1215.9 102.5 %all-reduce.5.cloned.1.call-start = ((), (), s32[]{:S(2)}) async-start(), calls=%async_computation.1 | async-start | bytes 4194304 | tf_op jit(solution)/shard_map/while/body/eval_jaxpr/psum | solution.py:81
  1320.3 16.0 collective-permute-start.1
  1336.2 99.7 %all-reduce.5.cloned.1.call-start = ((), (), s32[]{:S(2)}) async-start(), calls=%async_computation.1 | async-start | bytes 4194304 | tf_op jit(solution)/shard_map/while/body/eval_jaxpr/psum | solution.py:81
  1437.8 16.0 collective-permute-start.1
  1453.8 99.7 %all-reduce.5.cloned.1.call-start = ((), (), s32[]{:S(2)}) async-start(), calls=%async_computation.1 | async-start | bytes 4194304 | tf_op jit(solution)/shard_map/while/body/eval_jaxpr/psum | solution.py:81
  1555.4 16.0 collective-permute-start.1
  1571.3 99.7 %all-reduce.5.cloned.1.call-start = ((), (), s32[]{:S(2)}) async-start(), calls=%async_computation.1 | async-start | bytes 4194304 | tf_op jit(solution)/shard_map/while/body/eval_jaxpr/psum | solution.py:81
  1672.9 16.0 collective-permute-start.1
  1688.9 99.7 %all-reduce.5.cloned.1.call-start = ((), (), s32[]{:S(2)}) async-start(), calls=%async_computation.1 | async-start | bytes 4194304 | tf_op jit(solution)/shard_map/while/body/eval_jaxpr/psum | solution.py:81
  1790.4 16.0 collective-permute-start.1
  1806.4 99.7 %all-reduce.5.cloned.1.call-start = ((), (), s32[]{:S(2)}) async-start(), calls=%async_computation.1 | async-start | bytes 4194304 | tf_op jit(solution)/shard_map/while/body/eval_jaxpr/psum | solution.py:81
  1908.0 16.0 collective-permute-start.1
  1923.9 99.7 %all-reduce.5.cloned.1.call-start = ((), (), s32[]{:S(2)}) async-start(), calls=%async_computation.1 | async-start | bytes 4194304 | tf_op jit(solution)/shard_map/while/body/eval_jaxpr/psum | solution.py:81
  2025.5 16.0 collective-permute-start.1
  2041.5 99.7 %all-reduce.5.cloned.1.call-start = ((), (), s32[]{:S(2)}) async-start(), calls=%async_computation.1 | async-start | bytes 4194304 | tf_op jit(solution)/shard_map/while/body/eval_jaxpr/psum | solution.py:81
  2143.0 16.0 collective-permute-start.1
  (40 other events, 324.2 us)
Sparse Core Ops, SparseCore 0:
  23.3 88.3 all-reduce.2
  135.7 96.6 all-reduce.2
  256.2 96.6 all-reduce.2
  376.9 96.6 all-reduce.2
  497.4 96.6 all-reduce.2
  618.0 96.6 all-reduce.2
  738.6 96.6 all-reduce.2
  859.3 96.6 all-reduce.2
  979.9 96.6 all-reduce.2
  1117.1 85.7 all-reduce.4
  1229.7 88.6 all-reduce.4
  1350.1 85.8 all-reduce.4
  1467.6 85.8 all-reduce.4
  1585.1 85.8 all-reduce.4
  1702.7 85.8 all-reduce.4
  1820.2 85.8 all-reduce.4
  1937.7 85.8 all-reduce.4
  2055.3 85.8 all-reduce.4
where the time goes:
time: 2170 us
  waiting for transfers between devices  1510 us (70%)
  matrix products  456 us (21%)
  other arithmetic  109 us (5%)
  loops' own time  25.6 us (1%)
  starting transfers between devices  24.2 us (1%)
    psum x9, waiting for transfers between devices, fwd_tick(): lax.psum(part_sum, 'model')  857 us
    psum x9, waiting for transfers between devices, bwd_tick(): lax.psum(part_sum, 'model')  650 us
    dot_general x9, matrix products, bwd_tick(): jnp.einsum('bf,bd->fd', layer_act[layer_pos], grad_h, preferred_element_t...  127 us
    dot_general x9, matrix products, bwd_tick(): jnp.einsum('bd,bf->df', layer_in[layer_pos], grad_pre, preferred_element_...  127 us
    dot_general x9, matrix products, fwd_tick(): jnp.dot(hidden, w_in_loc[layer_pos], preferred_element_type=jnp.float32)  68.9 us
    dot_general x9, matrix products, bwd_tick(): jnp.einsum('bd,fd->bf', grad_h, w_out_loc[layer_pos], preferred_element_t...  64.4 us
    dynamic_update_slice x18, other arithmetic, stage_step(): lax.scan(fwd_tick, fwd_init, jnp.arange(num_ticks))  57.2 us
  transfers between devices with their start and end apart: 36, of which 18 were waited for; matrix products, arithmetic and copies ran while one was open for 13% of the time, Pallas kernels for 0%

commit v1 on v0

v1 whole, which is shorter than its diff:
```python
import functools

import jax
import jax.numpy as jnp
from jax import lax
from jax.experimental import pallas as pl
from jax.experimental.pallas import tpu as pltpu
from jax.sharding import PartitionSpec as P

GELU_COEF = 0.7978845608028654
CUBIC_COEF = 0.044715

CHUNK_TOKENS = 128
PIECE_COLS = 256
HIDDEN_COLS = 512
HOP_LAG = 2
SEND_SLOTS = 4
RECV_SLOTS = 8
GATHER_SLOTS = 16

BF16 = jnp.bfloat16
F32 = jnp.float32
MESH = pl.DeviceIdType.MESH


def gelu_tanh(values):
    inner_arg = GELU_COEF * (values + CUBIC_COEF * values * values * values)
    return 0.5 * values * (1.0 + jnp.tanh(inner_arg))


def gelu_slope(values):
    tanh_val = jnp.tanh(GELU_COEF * (values + CUBIC_COEF * values * values * values))
    return 0.5 * (1.0 + tanh_val) + 0.5 * values * (1.0 - tanh_val * tanh_val) * GELU_COEF * (1.0 + 3.0 * CUBIC_COEF * values * values)


def dot_nn(left, right):
    return jnp.dot(left, right, preferred_element_type=F32)


def dot_nt(left, right):
    return lax.dot_general(left, right, (((1,), (1,)), ((), ())), preferred_element_type=F32)


def stage_kernel(
    n_stage, n_model, n_chunk, half_pieces, piece, hid_cols, hop, grad_scale,
    inputs_hbm, targets_hbm, w1_hbm, w2_hbm,
    x_out, e_out, a_out, g_out, loss_out,
    w1, w2, acts, hid, send_buf, recv_buf, loss_acc, loss_in,
    w_sem, in_sem, tgt_sem, sum_send, sum_recv, gat_send, gat_recv, fwd_send, out_sem, loss_send, loss_recv, spent_sem,
):
    pos = lax.axis_index("model")
    stage = lax.axis_index("stage")
    last_pos = n_model - 1
    last_stage = n_stage - 1
    total = n_chunk * half_pieces
    half = half_pieces * piece
    drain = 6 * hop + SEND_SLOTS
    gap = jnp.where(stage == last_stage, max(0, 6 * hop + half_pieces - total), drain)
    hid_steps = w1.shape[1] // hid_cols

    barrier = pltpu.get_barrier_semaphore()
    for to_stage in range(n_stage):
        for to_pos in range(n_model):

            @pl.when((to_stage != stage) | (to_pos != pos))
            def _():
                pl.semaphore_signal(barrier, inc=1, device_id={"stage": to_stage, "model": to_pos}, device_id_type=MESH)

    copy_w1 = pltpu.make_async_copy(w1_hbm, w1, w_sem.at[0])
    copy_w2 = pltpu.make_async_copy(w2_hbm, w2, w_sem.at[1])

    def copy_in(chunk):
        return pltpu.make_async_copy(inputs_hbm.at[chunk], acts.at[0, chunk], in_sem.at[chunk])

    def grad_in(chunk):
        return pltpu.make_async_copy(inputs_hbm.at[chunk], acts.at[1, chunk], in_sem.at[n_chunk + chunk])

    def copy_targets(side):
        cols = pl.ds(side * half, half)
        return pltpu.make_async_copy(targets_hbm.at[:, :, cols], acts.at[1, :, :, cols], tgt_sem)

    def copy_out(kind, chunk):
        src, dst = ((acts.at[0], x_out), (acts.at[1], e_out), (hid.at[0], a_out), (hid.at[1], g_out))[kind]
        return pltpu.make_async_copy(src.at[chunk], dst.at[chunk], out_sem.at[kind, chunk])

    @pl.when(stage == 0)
    def _():
        copy_in(0).start()

    copy_w1.start()
    copy_w2.start()

    @pl.when(stage == 0)
    def _():
        for chunk in range(1, n_chunk):
            copy_in(chunk).start()

    @pl.when((stage == last_stage) & (pos == last_pos))
    def _():
        copy_targets(0).start()

    @pl.when((stage == last_stage) & (pos == 0))
    def _():
        copy_targets(1).start()

    loss_acc[...] = jnp.zeros_like(loss_acc)
    pl.semaphore_wait(barrier, n_stage * n_model - 1)

    def first_product(step):
        back = step - total - gap

        @pl.when((step < total) & (step % half_pieces == 0))
        def _():
            chunk = step // half_pieces
            copy_in(chunk).wait()
            copy_out(0, chunk).start()

            @pl.when(step == 0)
            def _():
                copy_w1.wait()

            def hid_step(index, carry):
                cols = pl.ds(pl.multiple_of(index * hid_cols, hid_cols), hid_cols)
                pre = dot_nn(acts[0, chunk], w1[:, cols]).astype(BF16)
                hid[1, chunk, :, cols] = pre
                hid[0, chunk, :, cols] = gelu_tanh(pre.astype(F32)).astype(BF16)
                return carry

            lax.fori_loop(0, hid_steps, hid_step, 0)
            copy_out(2, chunk).start()

            @pl.when(step == 0)
            def _():
                copy_w2.wait()

        @pl.when((back >= 0) & (back < total) & (back % half_pieces == 0))
        def _():
            chunk = back // half_pieces

            @pl.when(stage < last_stage)
            def _():
                @pl.when(back == 0)
                def _():
                    for side in (0, 1):
                        pl.semaphore_signal(spent_sem.at[side], inc=1, device_id={"stage": stage + 1}, device_id_type=MESH)

                grad_in(chunk).wait()

            copy_out(1, chunk).start()

            @pl.when(back == 0)
            def _():
                for done in range(n_chunk):
                    copy_out(0, done).wait()

            def hid_step(index, carry):
                cols = pl.ds(pl.multiple_of(index * hid_cols, hid_cols), hid_cols)
                grad_act = dot_nt(acts[1, chunk], w2[cols, :]).astype(BF16)
                slope = gelu_slope(hid[1, chunk, :, cols].astype(F32))
                hid[1, chunk, :, cols] = (slope * grad_act.astype(F32)).astype(BF16)
                return carry

            lax.fori_loop(0, hid_steps, hid_step, 0)
            copy_out(3, chunk).start()

    def send_loss(side):
        loss_in[side] = loss_acc[...]
        for to_stage in range(n_stage):
            for to_pos in range(n_model):

                @pl.when((to_stage != stage) | (to_pos != pos))
                def _():
                    loss_copy(side, to_stage, to_pos).start()

    def loss_copy(side, to_stage, to_pos):
        return pltpu.make_async_remote_copy(
            src_ref=loss_acc,
            dst_ref=loss_in.at[side],
            send_sem=loss_send.at[to_stage * n_model + to_pos],
            recv_sem=loss_recv.at[side],
            device_id={"stage": to_stage, "model": to_pos},
            device_id_type=MESH,
        )

    def turn(place):
        back = place - total - gap
        fwd = (place >= 0) & (place < total)
        bwd = (back >= 0) & (back < total) & (stage > 0)
        old = (place >= SEND_SLOTS) & (place < total + SEND_SLOTS)
        old_b = (back >= SEND_SLOTS) & (back < total + SEND_SLOTS) & (stage > 0)
        is_back = (back >= 0).astype(jnp.int32)
        return fwd, bwd, old, old_b, is_back, place - is_back * (total + gap)

    def piece_at(side, index):
        col = side * half + (index % half_pieces) * piece
        return index // half_pieces, pl.ds(pl.multiple_of(col, piece), piece)

    def sum_step(side, step):
        rank = pos if side == 0 else last_pos - pos
        nxt = pos + 1 if side == 0 else pos - 1
        place = step - hop * rank
        fwd, bwd, old, old_b, is_back, index = turn(place)
        out = lax.rem(place + 8 * SEND_SLOTS, SEND_SLOTS)
        inn = lax.rem(place + 8 * RECV_SLOTS, RECV_SLOTS)
        chunk, cols = piece_at(side, index)

        def hand_on():
            return pltpu.make_async_remote_copy(
                src_ref=send_buf.at[side, out],
                dst_ref=recv_buf.at[side, inn],
                send_sem=sum_send.at[side, out],
                recv_sem=sum_recv.at[side, inn],
                device_id={"model": nxt},
                device_id_type=MESH,
            )

        @pl.when((old | old_b) & (rank < last_pos))
        def _():
            hand_on().wait_send()

        @pl.when(fwd)
        def _():
            send_buf[side, out] = dot_nn(hid[0, chunk], w2[:, cols])

        @pl.when(bwd)
        def _():
            send_buf[side, out] = dot_nt(hid[1, chunk], w1[cols, :])

        @pl.when(fwd | bwd)
        def _():
            @pl.when(rank > 0)
            def _():
                hand_on().wait_recv()
                send_buf[side, out] = send_buf[side, out] + recv_buf[side, inn]

            @pl.when(rank < last_pos)
            def _():
                hand_on().start()

            @pl.when(rank == last_pos)
            def _():
                whole = acts[is_back, chunk, :, cols].astype(F32) + send_buf[side, out]
                scored = fwd & (stage == last_stage)

                @pl.when(scored)
                def _():
                    @pl.when(index == 0)
                    def _():
                        copy_targets(side).wait()

                    err = whole.astype(BF16).astype(F32) - acts[1, chunk, :, cols].astype(F32)
                    acts[1, chunk, :, cols] = (err * grad_scale).astype(BF16)
                    square = jnp.sum((err * err).reshape(err.shape[0] // 8, 8, piece), axis=0)
                    part = square[:, :128]
                    for lane in range(1, piece // 128):
                        part = part + square[:, lane * 128 : (lane + 1) * 128]
                    loss_acc[...] = loss_acc[...] + part

                    @pl.when(index == total - 1)
                    def _():
                        send_loss(side)

                @pl.when(jnp.logical_not(scored))
                def _():
                    acts[1 - is_back, chunk, :, cols] = whole.astype(BF16)

    def gather_step(side, step):
        rank = pos if side == 0 else last_pos - pos
        nxt = pos - 1 if side == 0 else pos + 1
        place = step - 3 * hop - hop * (last_pos - rank)
        fwd, bwd, old, old_b, is_back, index = turn(place)
        out = lax.rem(place + 8 * SEND_SLOTS, SEND_SLOTS)
        inn = lax.rem(place + 8 * GATHER_SLOTS, GATHER_SLOTS)
        chunk, cols = piece_at(side, index)

        def hand_on():
            return pltpu.make_async_remote_copy(
                src_ref=acts.at[1 - is_back, chunk, :, cols],
                dst_ref=acts.at[1 - is_back, chunk, :, cols],
                send_sem=gat_send.at[side, out],
                recv_sem=gat_recv.at[side, inn],
                device_id={"model": nxt},
                device_id_type=MESH,
            )

        def hand_over():
            return pltpu.make_async_remote_copy(
                src_ref=acts.at[1 - is_back, chunk, :, cols],
                dst_ref=acts.at[is_back, chunk, :, cols],
                send_sem=fwd_send.at[side, out],
                recv_sem=in_sem.at[is_back * n_chunk + chunk],
                device_id={"stage": stage + 1 - 2 * is_back},
                device_id_type=MESH,
            )

        def spent():
            return pltpu.make_async_remote_copy(
                src_ref=acts.at[0, 0, :, pl.ds(0, piece)],
                dst_ref=acts.at[0, 0, :, pl.ds(0, piece)],
                send_sem=gat_send.at[side, out],
                recv_sem=gat_recv.at[side, inn],
                device_id={"model": nxt},
                device_id_type=MESH,
            )

        def spent_over():
            return pltpu.make_async_remote_copy(
                src_ref=acts.at[0, 0, :, pl.ds(0, piece)],
                dst_ref=acts.at[0, 0, :, pl.ds(0, piece)],
                send_sem=fwd_send.at[side, out],
                recv_sem=gat_recv.at[side, inn],
                device_id={"model": nxt},
                device_id_type=MESH,
            )

        @pl.when((old | old_b) & (rank > 0))
        def _():
            spent().wait_send()

        @pl.when((old & (stage < last_stage)) | old_b)
        def _():
            spent_over().wait_send()

        @pl.when(fwd | bwd)
        def _():
            @pl.when(rank < last_pos)
            def _():
                hand_on().wait_recv()

            @pl.when(rank > 0)
            def _():
                hand_on().start()

            @pl.when(bwd & (index == total - half_pieces))
            def _():
                pl.semaphore_wait(spent_sem.at[side], 1)

            @pl.when(bwd | (stage < last_stage))
            def _():
                hand_over().start()

    def loop_step(step, carry):
        first_product(step)
        sum_step(0, step)
        sum_step(1, step)
        gather_step(0, step)
        gather_step(1, step)
        return carry

    lax.fori_loop(0, 2 * total + 2 * drain, loop_step, 0)

    for side, owner in ((0, last_pos), (1, 0)):
        owns = (stage == last_stage) & (pos == owner)

        @pl.when(jnp.logical_not(owns))
        def _():
            loss_copy(side, 0, 0).wait_recv()

        @pl.when(owns)
        def _():
            for to_stage in range(n_stage):
                for to_pos in range(n_model):

                    @pl.when((to_stage != stage) | (to_pos != pos))
                    def _():
                        loss_copy(side, to_stage, to_pos).wait_send()

    loss_out[...] = jnp.full(loss_out.shape, jnp.sum(loss_in[0] + loss_in[1]) * (0.5 * grad_scale), F32)
    for chunk in range(n_chunk):
        for kind in (1, 2, 3):
            copy_out(kind, chunk).wait()


def solution(mesh):
    n_stage = mesh.shape["stage"]
    n_model = mesh.shape["model"]

    def stage_step(inputs, targets, w_in, w_out):
        num_micro, num_tokens, model_dim = inputs.shape
        hid_dim = w_in.shape[3]
        rows = num_micro * num_tokens
        chunk = min(CHUNK_TOKENS, num_tokens)
        n_chunk = rows // chunk
        piece = min(PIECE_COLS, model_dim // 2)
        half_pieces = model_dim // 2 // piece
        hid_cols = min(HIDDEN_COLS, hid_dim)
        grad_scale = 1.0 / (rows * model_dim)
        kernel = functools.partial(
            stage_kernel, n_stage, n_model, n_chunk, half_pieces, piece, hid_cols, HOP_LAG, grad_scale
        )
        any_space = pl.BlockSpec(memory_space=pl.ANY)
        dma = pltpu.SemaphoreType.DMA
        layer_in, layer_grad, layer_act, layer_pre, loss = pl.pallas_call(
            kernel,
            out_shape=(
                jax.ShapeDtypeStruct((n_chunk, chunk, model_dim), BF16),
                jax.ShapeDtypeStruct((n_chunk, chunk, model_dim), BF16),
                jax.ShapeDtypeStruct((n_chunk, chunk, hid_dim), BF16),
                jax.ShapeDtypeStruct((n_chunk, chunk, hid_dim), BF16),
                jax.ShapeDtypeStruct((8, 128), F32),
            ),
            in_specs=[any_space] * 4,
            out_specs=(any_space, any_space, any_space, any_space, pl.BlockSpec(memory_space=pltpu.VMEM)),
            scratch_shapes=[
                pltpu.VMEM((model_dim, hid_dim), BF16),
                pltpu.VMEM((hid_dim, model_dim), BF16),
                pltpu.VMEM((2, n_chunk, chunk, model_dim), BF16),
                pltpu.VMEM((2, n_chunk, chunk, hid_dim), BF16),
                pltpu.VMEM((2, SEND_SLOTS, chunk, piece), F32),
                pltpu.VMEM((2, RECV_SLOTS, chunk, piece), F32),
                pltpu.VMEM((8, 128), F32),
                pltpu.VMEM((2, 8, 128), F32),
                dma((2,)),
                dma((2 * n_chunk,)),
                dma,
                dma((2, SEND_SLOTS)),
                dma((2, RECV_SLOTS)),
                dma((2, SEND_SLOTS)),
                dma((2, GATHER_SLOTS)),
                dma((2, SEND_SLOTS)),
                dma((4, n_chunk)),
                dma((n_stage * n_model,)),
                dma((2,)),
                pltpu.SemaphoreType.REGULAR((2,)),
            ],
            compiler_params=pltpu.CompilerParams(collective_id=0, has_side_effects=True, vmem_limit_bytes=62 * 1024 * 1024),
            name="stage_kernel",
        )(
            inputs.reshape(n_chunk, chunk, model_dim),
            targets.reshape(n_chunk, chunk, model_dim),
            w_in.reshape(model_dim, hid_dim),
            w_out.reshape(hid_dim, model_dim),
        )

        def over_rows(left, right):
            left = left.reshape(rows, left.shape[2])
            right = right.reshape(rows, right.shape[2])
            return lax.dot_general(left, right, (((0,), (0,)), ((), ())), preferred_element_type=F32)

        grad_in = over_rows(layer_in, layer_pre)
        grad_out = over_rows(layer_act, layer_grad)
        return grad_in[None, None], grad_out[None, None], loss[0, :1]

    return jax.shard_map(
        stage_step,
        mesh=mesh,
        in_specs=(P("data", None, None), P("data", None, None), P("stage", None, None, "model"), P("stage", None, "model", None)),
        out_specs=(P(("data", "stage"), None, None, "model"), P(("data", "stage"), None, "model", None), P("data")),
        check_vma=False,
    )
```

time: 2170 us -> 676 us (0.31)
  waiting for transfers between devices: 1510 us -> 0 us
  Pallas kernels: 0 us -> 637 us
  matrix products: 456 us -> 37 us
  other arithmetic: 109 us -> 0 us
  loops' own time: 25.6 us -> 0 us
  starting transfers between devices: 24.2 us -> 0 us
    psum x18 -> x0, waiting for transfers between devices: 1510 us -> none  [the longest x9 857 us: fwd_tick(): lax.psum(part_sum, 'model')]
    pallas_call x0 -> x1, Pallas kernels: none -> 637 us  [stage_step(): pl.pallas_call(kernel, out_shape=(jax.ShapeDtypeStruct((n_chunk, chunk, m...]
    dot_general x54 -> x2, matrix products: 456 us -> 37 us  [over_rows(): lax.dot_general(left, right, (((0,), (0,)), ((), ())), preferred_element_...]
    dynamic_update_slice x18 -> x0, other arithmetic: 57.2 us -> none  [stage_step(): lax.scan(fwd_tick, fwd_init, jnp.arange(num_ticks))]
    another operation x2 -> x0, loops' own time: 25.6 us -> none  [the longest x1 19.1 us: stage_step(): lax.scan(fwd_tick, fwd_init, jnp.arange(num_ticks))]
    ppermute x18 -> x0, starting transfers between devices: 23.7 us -> none  [the longest x9 12.1 us: fwd_tick(): sent_act = lax.ppermute(hidden, 'stage', down_perm)]
  transfers between devices with their start and end apart: 36 -> 0, of which waited for: 18 -> 0; matrix products, arithmetic and copies ran while one was open for 13% -> 0% of each run, Pallas kernels for 0% -> 0%
where the time goes in v1:
time: 676 us
  Pallas kernels  637 us (94%)
  matrix products  37 us (5%)
    pallas_call x1, Pallas kernels, stage_step(): pl.pallas_call(kernel, out_shape=(jax.ShapeDtypeStruct((n_chunk, chunk, m...  637 us
    dot_general x2, matrix products, over_rows(): lax.dot_general(left, right, (((0,), (0,)), ((), ())), preferred_element_...  37 us

profile of v1, /device:TPU:0, one launch (start us, length us, event | category | flops | bytes accessed | tf_op | source)
XLA Modules:
  0.0 675.8 jit_solution(835258836136279000)
XLA Ops:
  0.6 637.0 %stage_kernel.1 = (bf16[12,128,2048]{2,1,0:T(8,128)(2,1)}, bf16[12,128,2048]{2,1,0:T(8,128)(2,1)}, bf16[12,128,2048]{2,1,0:T(8,128)(2,1)}, bf16[12,128,2048]{2,1,0:T(8,128)(2,1)}, f32[8,128]{1,0:T(8,128)}) custom-call(bf16[12,128,2048]{2,1,0:T(8,128)(2,1)} %bitcast.19, bf16[12,128,2048]{2,1,0:T(8,128)(2,1)} %bitcast.20, bf16[2048,2048]{1,0:T(8,128)(2,1)} %bitcast.17, ...), custom_call_target="tpu_custom_call" | custom-call | tf_op jit(solution)/shard_map/stage_kernel/pallas_call | solution.py:393
  637.6 1.2 slice.3
  638.8 0.0 copy-start
  638.8 0.0 copy-start.1
  638.8 20.8 %convolution_bitcast_fusion.1 = f32[1,1,2048,2048]{3,2,1,0:T(8,128)} fusion(bf16[12,128,2048]{2,1,0:T(8,128)(2,1)} %get-tuple-element.8, bf16[12,128,2048]{2,1,0:T(8,128)(2,1)} %get-tuple-element.9), kind=kOutput, calls=%fused_computation.1 | convolution fusion | flops 12884901888 | bytes 29360128 | tf_op jit(solution)/shard_map/dot_general | solution.py:438
  659.7 0.0 copy-done
  659.7 0.0 copy-done.1
  659.7 16.2 %convolution_bitcast_fusion = f32[1,1,2048,2048]{3,2,1,0:T(8,128)} fusion(bf16[12,128,2048]{2,1,0:T(8,128)(2,1)S(1)} %copy-done.1, bf16[12,128,2048]{2,1,0:T(8,128)(2,1)S(1)} %copy-done), kind=kOutput, calls=%fused_computation | convolution fusion | flops 12884901888 | bytes 29360128 | tf_op jit(solution)/shard_map/dot_general | solution.py:438
Async XLA Ops:
  638.8 20.8 %copy-start = (bf16[12,128,2048]{2,1,0:T(8,128)(2,1)S(1)}, bf16[12,128,2048]{2,1,0:T(8,128)(2,1)}, u32[]{:S(2)}) copy-start(bf16[12,128,2048]{2,1,0:T(8,128)(2,1)} %get-tuple-element.11) | copy-start | bytes 18874372
  638.8 20.8 %copy-start.1 = (bf16[12,128,2048]{2,1,0:T(8,128)(2,1)S(1)}, bf16[12,128,2048]{2,1,0:T(8,128)(2,1)}, u32[]{:S(2)}) copy-start(bf16[12,128,2048]{2,1,0:T(8,128)(2,1)} %get-tuple-element.10) | copy-start | bytes 18874372

commit v2 on v1

v2 whole, which is shorter than its diff:
```python
import functools

import jax
import jax.numpy as jnp
from jax import lax
from jax.experimental import pallas as pl
from jax.experimental.pallas import tpu as pltpu
from jax.sharding import PartitionSpec as P

GELU_COEF = 0.7978845608028654
CUBIC_COEF = 0.044715

CHUNK_TOKENS = 64
PIECE_COLS = 256
HIDDEN_COLS = 512
PARTS = 2
HOP_LAG = 2
RECV_SLOTS = 8
LAST_LEAD = 5
PREV_LEAD = 16
FIRST_IDLE = 11
NEXT_IDLE = 7

BF16 = jnp.bfloat16
F32 = jnp.float32
MESH = pl.DeviceIdType.MESH


def gelu_tanh(values):
    inner_arg = GELU_COEF * (values + CUBIC_COEF * values * values * values)
    return 0.5 * values * (1.0 + jnp.tanh(inner_arg))


def gelu_slope(values):
    tanh_val = jnp.tanh(GELU_COEF * (values + CUBIC_COEF * values * values * values))
    return 0.5 * (1.0 + tanh_val) + 0.5 * values * (1.0 - tanh_val * tanh_val) * GELU_COEF * (1.0 + 3.0 * CUBIC_COEF * values * values)


def dot_nn(left, right):
    return jnp.dot(left, right, preferred_element_type=F32)


def dot_nt(left, right):
    return lax.dot_general(left, right, (((1,), (1,)), ((), ())), preferred_element_type=F32)


def stage_kernel(
    n_stage, n_model, n_chunk, half_pieces, piece, hop, lead, idle, grad_scale,
    inputs_hbm, targets_hbm, w1_hbm, w2_hbm,
    x_out, e_out, a_out, g_out, loss_out,
    wts, acts, hid, send_buf, recv_buf, loss_acc, loss_in,
    w_sem, in_sem, tgt_sem, sum_send, sum_recv, gat_send, gat_recv, over_send, back_send, back_recv, down_send, out_sem,
    loss_send, loss_recv, spent_sem,
):
    pos = lax.axis_index("model")
    stage = lax.axis_index("stage")
    last_pos = n_model - 1
    last_stage = n_stage - 1
    slots = half_pieces
    total = n_chunk * half_pieces
    half = half_pieces * piece
    hid_dim = wts.shape[2]
    hid_part = hid_dim // PARTS
    hid_cols = min(HIDDEN_COLS, hid_part)
    n_lead, n_idle = jnp.int32(n_chunk), jnp.int32(0)
    for at in range(n_stage):
        n_lead = jnp.where(stage == at, lead[at], n_lead)
        n_idle = jnp.where(stage == at, idle[at], n_idle)
    turns = 2 * n_chunk + n_idle
    early = half_pieces + 3 * hop

    barrier = pltpu.get_barrier_semaphore()
    for to_stage in range(n_stage):
        for to_pos in range(n_model):

            @pl.when((to_stage != stage) | (to_pos != pos))
            def _():
                pl.semaphore_signal(barrier, inc=1, device_id={"stage": to_stage, "model": to_pos}, device_id_type=MESH)

    copy_w1 = pltpu.make_async_copy(w1_hbm, wts.at[0], w_sem.at[0])
    copy_w2 = pltpu.make_async_copy(w2_hbm, wts.at[1], w_sem.at[1])

    def copy_in(chunk):
        return pltpu.make_async_copy(inputs_hbm.at[chunk], acts.at[0, chunk], in_sem.at[chunk])

    def copy_targets(side):
        cols = pl.ds(side * half, half)
        return pltpu.make_async_copy(targets_hbm.at[:, :, cols], acts.at[1, :, :, cols], tgt_sem)

    def copy_out(kind, chunk):
        src, dst = ((acts.at[0], x_out), (acts.at[1], e_out), (hid.at[0], a_out), (hid.at[1], g_out))[kind]
        return pltpu.make_async_copy(src.at[chunk], dst.at[chunk], out_sem.at[kind, chunk])

    @pl.when(stage == 0)
    def _():
        copy_in(0).start()

    copy_w1.start()
    copy_w2.start()

    @pl.when(stage == 0)
    def _():
        def start_in(chunk, carry):
            copy_in(chunk).start()
            return carry

        lax.fori_loop(1, n_chunk, start_in, 0)

    @pl.when((stage == last_stage) & (pos == last_pos))
    def _():
        copy_targets(0).start()

    @pl.when((stage == last_stage) & (pos == 0))
    def _():
        copy_targets(1).start()

    def transpose_weights():
        tile = min(256, hid_dim)
        count = hid_dim // tile

        def one(index, carry):
            rows = pl.ds(pl.multiple_of((index // count) * tile, tile), tile)
            cols = pl.ds(pl.multiple_of((index % count) * tile, tile), tile)
            wts[2, cols, rows] = jnp.swapaxes(wts[1, rows, cols], 0, 1)
            wts[3, cols, rows] = jnp.swapaxes(wts[0, rows, cols], 0, 1)
            return carry

        lax.fori_loop(0, count * count, one, 0)

    loss_acc[...] = jnp.zeros_like(loss_acc)
    copy_w1.wait()

    @pl.when(stage > 0)
    def _():
        copy_w2.wait()
        transpose_weights()

    pl.semaphore_wait(barrier, n_stage * n_model - 1)

    def turn_at(place):
        inside = (place >= 0) & (place < turns * half_pieces)
        place = jnp.clip(place, 0, turns * half_pieces - 1)
        turn = place // half_pieces
        after = turn - n_lead - n_idle
        mixed = after < 2 * (n_chunk - n_lead)
        pair = jnp.maximum(after, 0) // 2
        odd = jnp.maximum(after, 0) - 2 * pair
        leads = turn < n_lead
        fwd = leads | ((after >= 0) & mixed & (odd == 1))
        bwd = (after >= 0) & jnp.logical_not(mixed & (odd == 1))
        chunk = jnp.where(leads, turn, jnp.where(mixed, pair + odd * n_lead, after - (n_chunk - n_lead)))
        chunk = jnp.clip(chunk, 0, n_chunk - 1)
        return inside & fwd, inside & bwd, chunk, chunk * half_pieces + place % half_pieces

    def piece_at(side, index):
        col = side * half + (index % half_pieces) * piece
        return pl.ds(pl.multiple_of(col, piece), piece)

    def remote(src, dst, send_sem, recv_sem, device):
        return pltpu.make_async_remote_copy(
            src_ref=src, dst_ref=dst, send_sem=send_sem, recv_sem=recv_sem, device_id=device, device_id_type=MESH
        )

    def left(send_sem, like):
        remote(like, like, send_sem, loss_recv.at[0], {"model": pos}).wait_send()

    any_piece = acts.at[0, 0, :, pl.ds(0, piece)]
    any_sum = send_buf.at[0, 0]

    def rank_of(side):
        return pos if side == 0 else last_pos - pos

    def up(side):
        return {"model": pos + 1 if side == 0 else pos - 1}

    def down(side):
        return {"model": pos - 1 if side == 0 else pos + 1}

    def first_product(step, part):
        place = step + PARTS - 1 - part
        fwd, bwd, chunk, index = turn_at(place)
        starts = (place >= 0) & (place % half_pieces == 0)

        @pl.when(starts & fwd)
        def _():
            if part == 0:
                copy_in(chunk).wait()
                copy_out(0, chunk).start()
            for col in range(part * hid_part, (part + 1) * hid_part, hid_cols):
                cols = pl.ds(col, hid_cols)
                pre = dot_nn(acts[0, chunk], wts[0, :, cols]).astype(BF16)
                hid[1, chunk, :, cols] = pre
                hid[0, chunk, :, cols] = gelu_tanh(pre.astype(F32)).astype(BF16)
            if part == PARTS - 1:
                copy_out(2, chunk).start()

                @pl.when((stage == 0) & (index == 0))
                def _():
                    copy_w2.wait()

        @pl.when(starts & bwd)
        def _():
            if part == 0:
                copy_out(1, chunk).start()
                copy_out(0, chunk).wait()
            for col in range(part * hid_part, (part + 1) * hid_part, hid_cols):
                cols = pl.ds(col, hid_cols)
                grad_act = dot_nn(acts[1, chunk], wts[2, :, cols]).astype(BF16)
                slope = gelu_slope(hid[1, chunk, :, cols].astype(F32))
                hid[1, chunk, :, cols] = (slope * grad_act.astype(F32)).astype(BF16)
            if part == PARTS - 1:
                copy_out(3, chunk).start()

        if part == 0:

            @pl.when((stage == 0) & (place == n_lead * half_pieces))
            def _():
                transpose_weights()

    def loss_copy(side, to_stage, to_pos):
        return remote(
            loss_acc, loss_in.at[side], loss_send.at[to_stage * n_model + to_pos], loss_recv.at[side],
            {"stage": to_stage, "model": to_pos},
        )

    def send_loss(side):
        loss_in[side] = loss_acc[...]
        for to_stage in range(n_stage):
            for to_pos in range(n_model):

                @pl.when((to_stage != stage) | (to_pos != pos))
                def _():
                    loss_copy(side, to_stage, to_pos).start()

    def sum_steps(step):
        now = []
        for side in (0, 1):
            rank = rank_of(side)
            place = step - hop * rank
            fwd, bwd, chunk, index = turn_at(place)
            old_fwd, old_bwd, _, _ = turn_at(place - slots)
            out = jnp.maximum(place, 0) % slots
            inn = jnp.maximum(place, 0) % RECV_SLOTS
            is_back = bwd.astype(jnp.int32)
            sums = fwd | (bwd & (stage > 0))
            now.append((rank, fwd, bwd, sums, is_back, chunk, index, out, inn, piece_at(side, index)))

            @pl.when((old_fwd | (old_bwd & (stage > 0))) & (rank < last_pos))
            def _():
                left(sum_send.at[side, out], any_sum)

            @pl.when(old_bwd & (stage > 0) & (rank == last_pos))
            def _():
                left(down_send.at[side, out], any_piece)

        @pl.when(now[0][3] | now[1][3])
        def _():
            for side in (0, 1):
                _, _, _, _, is_back, chunk, _, out, _, cols = now[side]
                send_buf[side, out] = dot_nn(hid[is_back, chunk], wts[1 + 2 * is_back, :, cols])

        for side in (0, 1):
            rank, fwd, bwd, sums, is_back, chunk, index, out, inn, cols = now[side]
            hand_on = remote(
                send_buf.at[side, out], recv_buf.at[side, inn], sum_send.at[side, out], sum_recv.at[side, inn], up(side)
            )

            @pl.when(sums & (rank > 0))
            def _():
                hand_on.wait_recv()
                send_buf[side, out] = send_buf[side, out] + recv_buf[side, inn]

            @pl.when(sums & (rank < last_pos))
            def _():
                hand_on.start()

            @pl.when(sums & (rank == last_pos))
            def _():
                whole = acts[is_back, chunk, :, cols].astype(F32) + send_buf[side, out]
                scored = fwd & (stage == last_stage)

                @pl.when(scored)
                def _():
                    @pl.when(index == 0)
                    def _():
                        copy_targets(side).wait()

                    err = whole.astype(BF16).astype(F32) - acts[1, chunk, :, cols].astype(F32)
                    acts[1, chunk, :, cols] = (err * grad_scale).astype(BF16)
                    square = jnp.sum((err * err).reshape(err.shape[0] // 8, 8, piece), axis=0)
                    part = square[:, :128]
                    for lane in range(1, piece // 128):
                        part = part + square[:, lane * 128 : (lane + 1) * 128]
                    loss_acc[...] = loss_acc[...] + part

                    @pl.when(index == total - 1)
                    def _():
                        send_loss(side)

                @pl.when(jnp.logical_not(scored))
                def _():
                    acts[1 - is_back, chunk, :, cols] = whole.astype(BF16)

                @pl.when(bwd & (index == total - half_pieces))
                def _():
                    pl.semaphore_wait(spent_sem.at[side], 1)

                @pl.when(bwd)
                def _():
                    remote(
                        acts.at[0, chunk, :, cols], acts.at[1, chunk, :, cols], down_send.at[side, out],
                        back_recv.at[side, index], {"stage": stage - 1},
                    ).start()

    def gather_step(side, step):
        rank = rank_of(side)
        place = step - 3 * hop - hop * (last_pos - rank)
        fwd, _, chunk, index = turn_at(place)
        old, _, _, old_index = turn_at(place - slots)
        out = jnp.maximum(place, 0) % slots
        cols = piece_at(side, index)
        here = acts.at[1, chunk, :, cols]
        hand_on = remote(here, here, gat_send.at[side, out], gat_recv.at[side, index], down(side))

        @pl.when(old & (rank > 0))
        def _():
            left(gat_send.at[side, out], any_piece)

        @pl.when(old & (stage < last_stage))
        def _():
            left(over_send.at[side, out], any_piece)

            @pl.when((old_index == total - 1) & (rank == last_pos))
            def _():
                pl.semaphore_signal(spent_sem.at[side], inc=1, device_id={"stage": stage + 1}, device_id_type=MESH)

        @pl.when(fwd & (rank < last_pos))
        def _():
            hand_on.wait_recv()

        @pl.when(fwd & (rank > 0))
        def _():
            hand_on.start()

        @pl.when(fwd & (stage < last_stage))
        def _():
            remote(here, acts.at[0, chunk, :, cols], over_send.at[side, out], in_sem.at[chunk], {"stage": stage + 1}).start()

    def back_step(side, step):
        rank = rank_of(side)
        place = step + early - hop * (last_pos - rank)
        _, bwd, chunk, index = turn_at(place)
        _, old, _, _ = turn_at(place - slots)
        out = jnp.maximum(place, 0) % slots
        here = acts.at[1, chunk, :, piece_at(side, index)]
        hand_on = remote(here, here, back_send.at[side, out], back_recv.at[side, index], down(side))

        @pl.when(old & (rank > 0) & (stage < last_stage))
        def _():
            left(back_send.at[side, out], any_piece)

        @pl.when(bwd & (stage < last_stage))
        def _():
            hand_on.wait_recv()

            @pl.when(rank > 0)
            def _():
                hand_on.start()

    def loop_step(step, carry):
        back_step(0, step)
        back_step(1, step)
        for part in range(PARTS):
            first_product(step, part)
        sum_steps(step)
        gather_step(0, step)
        gather_step(1, step)
        return carry

    lax.fori_loop(1 - PARTS, (2 * n_chunk + max(idle)) * half_pieces + 6 * hop + slots, loop_step, 0)

    for side, owner in ((0, last_pos), (1, 0)):
        owns = (stage == last_stage) & (pos == owner)

        @pl.when(jnp.logical_not(owns))
        def _():
            loss_copy(side, 0, 0).wait_recv()

        @pl.when(owns)
        def _():
            for to_stage in range(n_stage):
                for to_pos in range(n_model):

                    @pl.when((to_stage != stage) | (to_pos != pos))
                    def _():
                        loss_copy(side, to_stage, to_pos).wait_send()

    loss_out[...] = jnp.full(loss_out.shape, jnp.sum(loss_in[0] + loss_in[1]) * (0.5 * grad_scale), F32)

    def end_out(chunk, carry):
        for kind in (1, 2, 3):
            copy_out(kind, chunk).wait()
        return carry

    lax.fori_loop(0, n_chunk, end_out, 0)


def solution(mesh):
    n_stage = mesh.shape["stage"]
    n_model = mesh.shape["model"]

    def stage_step(inputs, targets, w_in, w_out):
        num_micro, num_tokens, model_dim = inputs.shape
        hid_dim = w_in.shape[3]
        rows = num_micro * num_tokens
        chunk = min(CHUNK_TOKENS, num_tokens)
        n_chunk = rows // chunk
        piece = min(PIECE_COLS, model_dim // 2)
        half_pieces = model_dim // 2 // piece
        grad_scale = 1.0 / (rows * model_dim)
        lead = [n_chunk] * (n_stage - 2) + [min(PREV_LEAD, n_chunk), min(LAST_LEAD, n_chunk)]
        idle = [FIRST_IDLE] + [NEXT_IDLE] * (n_stage - 3) + [0, 0]
        kernel = functools.partial(stage_kernel, n_stage, n_model, n_chunk, half_pieces, piece, HOP_LAG, lead, idle, grad_scale)
        any_space = pl.BlockSpec(memory_space=pl.ANY)
        dma = pltpu.SemaphoreType.DMA
        layer_in, layer_grad, layer_act, layer_pre, loss = pl.pallas_call(
            kernel,
            out_shape=(
                jax.ShapeDtypeStruct((n_chunk, chunk, model_dim), BF16),
                jax.ShapeDtypeStruct((n_chunk, chunk, model_dim), BF16),
                jax.ShapeDtypeStruct((n_chunk, chunk, hid_dim), BF16),
                jax.ShapeDtypeStruct((n_chunk, chunk, hid_dim), BF16),
                jax.ShapeDtypeStruct((8, 128), F32),
            ),
            in_specs=[any_space] * 4,
            out_specs=(any_space, any_space, any_space, any_space, pl.BlockSpec(memory_space=pltpu.VMEM)),
            scratch_shapes=[
                pltpu.VMEM((4, model_dim, hid_dim), BF16),
                pltpu.VMEM((2, n_chunk, chunk, model_dim), BF16),
                pltpu.VMEM((2, n_chunk, chunk, hid_dim), BF16),
                pltpu.VMEM((2, half_pieces, chunk, piece), F32),
                pltpu.VMEM((2, RECV_SLOTS, chunk, piece), F32),
                pltpu.VMEM((8, 128), F32),
                pltpu.VMEM((2, 8, 128), F32),
                dma((2,)),
                dma((n_chunk,)),
                dma,
                dma((2, half_pieces)),
                dma((2, RECV_SLOTS)),
                dma((2, half_pieces)),
                dma((2, n_chunk * half_pieces)),
                dma((2, half_pieces)),
                dma((2, half_pieces)),
                dma((2, n_chunk * half_pieces)),
                dma((2, half_pieces)),
                dma((4, n_chunk)),
                dma((n_stage * n_model,)),
                dma((2,)),
                pltpu.SemaphoreType.REGULAR((2,)),
            ],
            compiler_params=pltpu.CompilerParams(collective_id=0, has_side_effects=True, vmem_limit_bytes=63 * 1024 * 1024),
            name="stage_kernel",
        )(
            inputs.reshape(n_chunk, chunk, model_dim),
            targets.reshape(n_chunk, chunk, model_dim),
            w_in.reshape(model_dim, hid_dim),
            w_out.reshape(hid_dim, model_dim),
        )

        def over_rows(left, right):
            left = left.reshape(rows, left.shape[2])
            right = right.reshape(rows, right.shape[2])
            return lax.dot_general(left, right, (((0,), (0,)), ((), ())), preferred_element_type=F32)

        grad_in = over_rows(layer_in, layer_pre)
        grad_out = over_rows(layer_act, layer_grad)
        return grad_in[None, None], grad_out[None, None], loss[0, :1]

    return jax.shard_map(
        stage_step,
        mesh=mesh,
        in_specs=(P("data", None, None), P("data", None, None), P("stage", None, None, "model"), P("stage", None, "model", None)),
        out_specs=(P(("data", "stage"), None, None, "model"), P(("data", "stage"), None, "model", None), P("data")),
        check_vma=False,
    )
```

time: 676 us -> 609 us (0.901)
  Pallas kernels: 637 us -> 570 us
    pallas_call x1, Pallas kernels: 637 us -> 570 us  [stage_step(): pl.pallas_call(kernel, out_shape=(jax.ShapeDtypeStruct((n_chunk, chunk, m...]
where the time goes in v2:
time: 609 us; the launch traced here: 608 us
  Pallas kernels  570 us (94%)
  matrix products  37 us (6%)
    pallas_call x1, Pallas kernels, stage_step(): pl.pallas_call(kernel, out_shape=(jax.ShapeDtypeStruct((n_chunk, chunk, m...  570 us
    dot_general x2, matrix products, over_rows(): lax.dot_general(left, right, (((0,), (0,)), ((), ())), preferred_element_...  37 us

profile of v2, /device:TPU:0, one launch (start us, length us, event | category | flops | bytes accessed | tf_op | source)
XLA Modules:
  0.0 608.5 jit_solution(9887001710810532049)
XLA Ops:
  0.6 569.6 %stage_kernel.1 = (bf16[24,64,2048]{2,1,0:T(8,128)(2,1)}, bf16[24,64,2048]{2,1,0:T(8,128)(2,1)}, bf16[24,64,2048]{2,1,0:T(8,128)(2,1)}, bf16[24,64,2048]{2,1,0:T(8,128)(2,1)}, f32[8,128]{1,0:T(8,128)}) custom-call(bf16[24,64,2048]{2,1,0:T(8,128)(2,1)} %bitcast.19, bf16[24,64,2048]{2,1,0:T(8,128)(2,1)} %bitcast.20, bf16[2048,2048]{1,0:T(8,128)(2,1)} %bitcast.17, ...), custom_call_target="tpu_custom_call" | custom-call | tf_op jit(solution)/shard_map/stage_kernel/pallas_call | solution.py:426
  570.2 1.2 slice.3
  571.4 0.0 copy-start
  571.4 0.0 copy-start.1
  571.4 20.8 %convolution_bitcast_fusion.1 = f32[1,1,2048,2048]{3,2,1,0:T(8,128)} fusion(bf16[24,64,2048]{2,1,0:T(8,128)(2,1)} %get-tuple-element.8, bf16[24,64,2048]{2,1,0:T(8,128)(2,1)} %get-tuple-element.9), kind=kOutput, calls=%fused_computation.1 | convolution fusion | flops 12884901888 | bytes 29360128 | tf_op jit(solution)/shard_map/dot_general | solution.py:473
  592.3 0.0 copy-done
  592.3 0.0 copy-done.1
  592.3 16.2 %convolution_bitcast_fusion = f32[1,1,2048,2048]{3,2,1,0:T(8,128)} fusion(bf16[24,64,2048]{2,1,0:T(8,128)(2,1)S(1)} %copy-done.1, bf16[24,64,2048]{2,1,0:T(8,128)(2,1)S(1)} %copy-done), kind=kOutput, calls=%fused_computation | convolution fusion | flops 12884901888 | bytes 29360128 | tf_op jit(solution)/shard_map/dot_general | solution.py:473
Async XLA Ops:
  571.4 20.8 %copy-start = (bf16[24,64,2048]{2,1,0:T(8,128)(2,1)S(1)}, bf16[24,64,2048]{2,1,0:T(8,128)(2,1)}, u32[]{:S(2)}) copy-start(bf16[24,64,2048]{2,1,0:T(8,128)(2,1)} %get-tuple-element.11) | copy-start | bytes 18874372
  571.4 20.8 %copy-start.1 = (bf16[24,64,2048]{2,1,0:T(8,128)(2,1)S(1)}, bf16[24,64,2048]{2,1,0:T(8,128)(2,1)}, u32[]{:S(2)}) copy-start(bf16[24,64,2048]{2,1,0:T(8,128)(2,1)} %get-tuple-element.10) | copy-start | bytes 18874372

commit v3 on v2

--- a/solution.py
+++ b/solution.py
@@ -60,6 +60,7 @@
     total = n_chunk * half_pieces
     half = half_pieces * piece
     hid_dim = wts.shape[2]
+    chunk_rows = acts.shape[2]
     hid_part = hid_dim // PARTS
     hid_cols = min(HIDDEN_COLS, hid_part)
     n_lead, n_idle = jnp.int32(n_chunk), jnp.int32(0)
@@ -67,6 +68,7 @@
         n_lead = jnp.where(stage == at, lead[at], n_lead)
         n_idle = jnp.where(stage == at, idle[at], n_idle)
     turns = 2 * n_chunk + n_idle
+    n_steps = turns * half_pieces + jnp.where(stage == 0, max(1 - half_pieces, -hop), 6 * hop + slots)
     early = half_pieces + 3 * hop
 
     barrier = pltpu.get_barrier_semaphore()
@@ -89,7 +91,8 @@
 
     def copy_out(kind, chunk):
         src, dst = ((acts.at[0], x_out), (acts.at[1], e_out), (hid.at[0], a_out), (hid.at[1], g_out))[kind]
-        return pltpu.make_async_copy(src.at[chunk], dst.at[chunk], out_sem.at[kind, chunk])
+        rows = pl.ds(pl.multiple_of(chunk * chunk_rows, chunk_rows), chunk_rows)
+        return pltpu.make_async_copy(src.at[chunk], dst.at[rows, :], out_sem.at[kind, chunk])
 
     @pl.when(stage == 0)
     def _():
@@ -137,23 +140,38 @@
 
     pl.semaphore_wait(barrier, n_stage * n_model - 1)
 
-    def turn_at(place):
-        inside = (place >= 0) & (place < turns * half_pieces)
-        place = jnp.clip(place, 0, turns * half_pieces - 1)
-        turn = place // half_pieces
-        after = turn - n_lead - n_idle
-        mixed = after < 2 * (n_chunk - n_lead)
-        pair = jnp.maximum(after, 0) // 2
-        odd = jnp.maximum(after, 0) - 2 * pair
-        leads = turn < n_lead
-        fwd = leads | ((after >= 0) & mixed & (odd == 1))
-        bwd = (after >= 0) & jnp.logical_not(mixed & (odd == 1))
-        chunk = jnp.where(leads, turn, jnp.where(mixed, pair + odd * n_lead, after - (n_chunk - n_lead)))
-        chunk = jnp.clip(chunk, 0, n_chunk - 1)
-        return inside & fwd, inside & bwd, chunk, chunk * half_pieces + place % half_pieces
+    n_mixed = 2 * (n_chunk - n_lead)
+    n_after = 2 * n_chunk - n_lead
+    n_first = n_lead + n_idle
+
+    def turn_of(place):
+        return lax.div(place + 64 * half_pieces, half_pieces) - 64
+
+    def is_fwd(turn):
+        after = turn - n_first
+        odd = lax.rem(after + 1024, 2) == 1
+        return ((turn >= 0) & (turn < n_lead)) | ((after >= 0) & (after < n_mixed) & odd)
+
+    def is_bwd(turn):
+        after = turn - n_first
+        odd = lax.rem(after + 1024, 2) == 1
+        return (after >= 0) & (after < n_after) & jnp.logical_not((after < n_mixed) & odd)
+
+    def fwd_chunk(turn):
+        return jnp.where(turn < n_lead, turn, n_lead + lax.div(turn - n_first + 1024, 2) - 512)
+
+    def bwd_chunk(turn):
+        after = turn - n_first
+        return jnp.where(after < n_mixed, lax.div(after + 1024, 2) - 512, after - (n_chunk - n_lead))
+
+    def piece_of(place):
+        return lax.rem(place + 64 * half_pieces, half_pieces)
+
+    def any_chunk(turn, bwd):
+        return jnp.clip(jnp.where(bwd, bwd_chunk(turn), fwd_chunk(turn)), 0, n_chunk - 1)
 
     def piece_at(side, index):
-        col = side * half + (index % half_pieces) * piece
+        col = side * half + index * piece
         return pl.ds(pl.multiple_of(col, piece), piece)
 
     def remote(src, dst, send_sem, recv_sem, device):
@@ -178,11 +196,12 @@
 
     def first_product(step, part):
         place = step + PARTS - 1 - part
-        fwd, bwd, chunk, index = turn_at(place)
-        starts = (place >= 0) & (place % half_pieces == 0)
-
-        @pl.when(starts & fwd)
-        def _():
+        turn = turn_of(place)
+        starts = piece_of(place) == 0
+
+        @pl.when(starts & is_fwd(turn))
+        def _():
+            chunk = fwd_chunk(turn)
             if part == 0:
                 copy_in(chunk).wait()
                 copy_out(0, chunk).start()
@@ -194,12 +213,13 @@
             if part == PARTS - 1:
                 copy_out(2, chunk).start()
 
-                @pl.when((stage == 0) & (index == 0))
+                @pl.when((stage == 0) & (turn == 0))
                 def _():
                     copy_w2.wait()
 
-        @pl.when(starts & bwd)
-        def _():
+        @pl.when(starts & is_bwd(turn))
+        def _():
+            chunk = bwd_chunk(turn)
             if part == 0:
                 copy_out(1, chunk).start()
                 copy_out(0, chunk).wait()
@@ -237,13 +257,14 @@
         for side in (0, 1):
             rank = rank_of(side)
             place = step - hop * rank
-            fwd, bwd, chunk, index = turn_at(place)
-            old_fwd, old_bwd, _, _ = turn_at(place - slots)
-            out = jnp.maximum(place, 0) % slots
-            inn = jnp.maximum(place, 0) % RECV_SLOTS
+            turn = turn_of(place)
+            fwd, bwd = is_fwd(turn), is_bwd(turn)
+            old_fwd, old_bwd = is_fwd(turn - 1), is_bwd(turn - 1)
+            out = piece_of(place)
+            inn = lax.rem(place + 64 * RECV_SLOTS, RECV_SLOTS)
             is_back = bwd.astype(jnp.int32)
             sums = fwd | (bwd & (stage > 0))
-            now.append((rank, fwd, bwd, sums, is_back, chunk, index, out, inn, piece_at(side, index)))
+            now.append((rank, fwd, bwd, sums, is_back, any_chunk(turn, bwd), out, inn, piece_at(side, out)))
 
             @pl.when((old_fwd | (old_bwd & (stage > 0))) & (rank < last_pos))
             def _():
@@ -256,11 +277,12 @@
         @pl.when(now[0][3] | now[1][3])
         def _():
             for side in (0, 1):
-                _, _, _, _, is_back, chunk, _, out, _, cols = now[side]
+                _, _, _, _, is_back, chunk, out, _, cols = now[side]
                 send_buf[side, out] = dot_nn(hid[is_back, chunk], wts[1 + 2 * is_back, :, cols])
 
         for side in (0, 1):
-            rank, fwd, bwd, sums, is_back, chunk, index, out, inn, cols = now[side]
+            rank, fwd, bwd, sums, is_back, chunk, out, inn, cols = now[side]
+            index = chunk * half_pieces + out
             hand_on = remote(
                 send_buf.at[side, out], recv_buf.at[side, inn], sum_send.at[side, out], sum_recv.at[side, inn], up(side)
             )
@@ -315,10 +337,12 @@
     def gather_step(side, step):
         rank = rank_of(side)
         place = step - 3 * hop - hop * (last_pos - rank)
-        fwd, _, chunk, index = turn_at(place)
-        old, _, _, old_index = turn_at(place - slots)
-        out = jnp.maximum(place, 0) % slots
-        cols = piece_at(side, index)
+        turn = turn_of(place)
+        fwd, old = is_fwd(turn), is_fwd(turn - 1)
+        out = piece_of(place)
+        chunk = jnp.clip(fwd_chunk(turn), 0, n_chunk - 1)
+        index = chunk * half_pieces + out
+        cols = piece_at(side, out)
         here = acts.at[1, chunk, :, cols]
         hand_on = remote(here, here, gat_send.at[side, out], gat_recv.at[side, index], down(side))
 
@@ -330,7 +354,7 @@
         def _():
             left(over_send.at[side, out], any_piece)
 
-            @pl.when((old_index == total - 1) & (rank == last_pos))
+            @pl.when((fwd_chunk(turn - 1) == n_chunk - 1) & (out == half_pieces - 1) & (rank == last_pos))
             def _():
                 pl.semaphore_signal(spent_sem.at[side], inc=1, device_id={"stage": stage + 1}, device_id_type=MESH)
 
@@ -349,10 +373,12 @@
     def back_step(side, step):
         rank = rank_of(side)
         place = step + early - hop * (last_pos - rank)
-        _, bwd, chunk, index = turn_at(place)
-        _, old, _, _ = turn_at(place - slots)
-        out = jnp.maximum(place, 0) % slots
-        here = acts.at[1, chunk, :, piece_at(side, index)]
+        turn = turn_of(place)
+        bwd, old = is_bwd(turn), is_bwd(turn - 1)
+        out = piece_of(place)
+        chunk = jnp.clip(bwd_chunk(turn), 0, n_chunk - 1)
+        index = chunk * half_pieces + out
+        here = acts.at[1, chunk, :, piece_at(side, out)]
         hand_on = remote(here, here, back_send.at[side, out], back_recv.at[side, index], down(side))
 
         @pl.when(old & (rank > 0) & (stage < last_stage))
@@ -377,7 +403,7 @@
         gather_step(1, step)
         return carry
 
-    lax.fori_loop(1 - PARTS, (2 * n_chunk + max(idle)) * half_pieces + 6 * hop + slots, loop_step, 0)
+    lax.fori_loop(1 - PARTS, n_steps, loop_step, 0)
 
     for side, owner in ((0, last_pos), (1, 0)):
         owns = (stage == last_stage) & (pos == owner)
@@ -426,10 +452,10 @@
         layer_in, layer_grad, layer_act, layer_pre, loss = pl.pallas_call(
             kernel,
             out_shape=(
-                jax.ShapeDtypeStruct((n_chunk, chunk, model_dim), BF16),
-                jax.ShapeDtypeStruct((n_chunk, chunk, model_dim), BF16),
-                jax.ShapeDtypeStruct((n_chunk, chunk, hid_dim), BF16),
-                jax.ShapeDtypeStruct((n_chunk, chunk, hid_dim), BF16),
+                jax.ShapeDtypeStruct((rows, model_dim), BF16),
+                jax.ShapeDtypeStruct((rows, model_dim), BF16),
+                jax.ShapeDtypeStruct((rows, hid_dim), BF16),
+                jax.ShapeDtypeStruct((rows, hid_dim), BF16),
                 jax.ShapeDtypeStruct((8, 128), F32),
             ),
             in_specs=[any_space] * 4,
@@ -468,8 +494,6 @@
         )
 
         def over_rows(left, right):
-            left = left.reshape(rows, left.shape[2])
-            right = right.reshape(rows, right.shape[2])
             return lax.dot_general(left, right, (((0,), (0,)), ((), ())), preferred_element_type=F32)
 
         grad_in = over_rows(layer_in, layer_pre)

time: 609 us -> 597 us (0.980)
  Pallas kernels: 570 us -> 558 us
    pallas_call x1, Pallas kernels: 570 us -> 558 us  [stage_step(): pl.pallas_call(kernel, out_shape=(jax.ShapeDtypeStruct((rows, model_dim),...]
where the time goes in v3:
time: 597 us
  Pallas kernels  558 us (93%)
  matrix products  37 us (6%)
    pallas_call x1, Pallas kernels, stage_step(): pl.pallas_call(kernel, out_shape=(jax.ShapeDtypeStruct((rows, model_dim),...  558 us
    dot_general x2, matrix products, over_rows(): lax.dot_general(left, right, (((0,), (0,)), ((), ())), preferred_element_...  37 us

profile of v3, /device:TPU:0, one launch (start us, length us, event | category | flops | bytes accessed | tf_op | source)
XLA Modules:
  0.0 596.8 jit_solution(18006819742749288342)
XLA Ops:
  0.6 557.9 %stage_kernel.1 = (bf16[1536,2048]{1,0:T(8,128)(2,1)}, bf16[1536,2048]{1,0:T(8,128)(2,1)}, bf16[1536,2048]{1,0:T(8,128)(2,1)}, bf16[1536,2048]{1,0:T(8,128)(2,1)}, f32[8,128]{1,0:T(8,128)}) custom-call(bf16[24,64,2048]{2,1,0:T(8,128)(2,1)} %bitcast.15, bf16[24,64,2048]{2,1,0:T(8,128)(2,1)} %bitcast.16, bf16[2048,2048]{1,0:T(8,128)(2,1)} %bitcast.13, ...), custom_call_target="tpu_custom_call" | custom-call | tf_op jit(solution)/shard_map/stage_kernel/pallas_call | solution.py:452
  558.6 1.2 slice.3
  559.8 0.0 copy-start
  559.8 0.0 copy-start.1
  559.8 20.8 %convolution_bitcast_fusion.1 = f32[1,1,2048,2048]{3,2,1,0:T(8,128)} fusion(bf16[1536,2048]{1,0:T(8,128)(2,1)} %get-tuple-element.8, bf16[1536,2048]{1,0:T(8,128)(2,1)} %get-tuple-element.9), kind=kOutput, calls=%fused_computation.1 | convolution fusion | flops 12884901888 | bytes 29360128 | tf_op jit(solution)/shard_map/dot_general | solution.py:497
  580.6 0.0 copy-done
  580.6 0.0 copy-done.1
  580.6 16.2 %convolution_bitcast_fusion = f32[1,1,2048,2048]{3,2,1,0:T(8,128)} fusion(bf16[1536,2048]{1,0:T(8,128)(2,1)S(1)} %copy-done.1, bf16[1536,2048]{1,0:T(8,128)(2,1)S(1)} %copy-done), kind=kOutput, calls=%fused_computation | convolution fusion | flops 12884901888 | bytes 29360128 | tf_op jit(solution)/shard_map/dot_general | solution.py:497
Async XLA Ops:
  559.8 20.8 %copy-start = (bf16[1536,2048]{1,0:T(8,128)(2,1)S(1)}, bf16[1536,2048]{1,0:T(8,128)(2,1)}, u32[]{:S(2)}) copy-start(bf16[1536,2048]{1,0:T(8,128)(2,1)} %get-tuple-element.11) | copy-start | bytes 18874372
  559.8 20.8 %copy-start.1 = (bf16[1536,2048]{1,0:T(8,128)(2,1)S(1)}, bf16[1536,2048]{1,0:T(8,128)(2,1)}, u32[]{:S(2)}) copy-start(bf16[1536,2048]{1,0:T(8,128)(2,1)} %get-tuple-element.10) | copy-start | bytes 18874372

commit v4 on v3

--- a/solution.py
+++ b/solution.py
@@ -16,6 +16,8 @@
 PARTS = 2
 HOP_LAG = 2
 RECV_SLOTS = 8
+GRAD_ROWS = 512
+GRAD_COLS = 1024
 LAST_LEAD = 5
 PREV_LEAD = 16
 FIRST_IDLE = 11
@@ -429,6 +431,122 @@
         return carry
 
     lax.fori_loop(0, n_chunk, end_out, 0)
+
+
+def grad_kernel(blk, cols, x_hbm, g_hbm, a_hbm, e_hbm, dw1, dw2, lhs, lhs_t, rhs, out, lhs_sem, rhs_sem, out_sem):
+    rows = lhs.shape[1]
+    n_blk = dw1.shape[0] // blk
+    n_col = dw1.shape[1] // cols
+
+    def copy_lhs(which, index, slot):
+        src = (x_hbm, a_hbm)[which]
+        return pltpu.make_async_copy(src.at[:, pl.ds(pl.multiple_of(index * blk, blk), blk)], lhs.at[slot], lhs_sem.at[slot])
+
+    def copy_rhs(which, index):
+        src = (g_hbm, e_hbm)[which]
+        part = pl.ds(index * cols, cols)
+        return pltpu.make_async_copy(src.at[:, part], rhs.at[which, :, part], rhs_sem.at[which, index])
+
+    def copy_res(which, index, col, slot):
+        dst = (dw1, dw2)[which]
+        return pltpu.make_async_copy(
+            out.at[slot], dst.at[pl.ds(pl.multiple_of(index * blk, blk), blk), pl.ds(col * cols, cols)], out_sem.at[slot]
+        )
+
+    copy_lhs(0, 0, 0).start()
+    for col in range(n_col):
+        copy_rhs(0, col).start()
+    copy_lhs(0, 1, 1).start()
+    for col in range(n_col):
+        copy_rhs(1, col).start()
+
+    def turn(slot, col):
+        width = blk // n_col
+        part = pl.ds(col * width, width)
+        lhs_t[slot, part, :] = jnp.swapaxes(lhs[slot, :, part], 0, 1)
+
+    copy_lhs(0, 0, 0).wait()
+    for col in range(n_col):
+        turn(0, col)
+
+    for which in (0, 1):
+
+        def pair(step, carry):
+            for slot in (0, 1):
+                index = 2 * step + slot
+                nxt = 1 - slot
+                if slot == 0:
+                    copy_lhs(which, index + 1, nxt).wait()
+                else:
+
+                    @pl.when(index + 1 < n_blk)
+                    def _():
+                        copy_lhs(which, index + 1, nxt).wait()
+
+                    if which == 0:
+
+                        @pl.when(index + 1 == n_blk)
+                        def _():
+                            copy_lhs(1, 0, nxt).wait()
+                for col in range(n_col):
+
+                    @pl.when(index == 0)
+                    def _():
+                        copy_rhs(which, col).wait()
+
+                    place = slot * n_col + col
+                    if which == 0:
+
+                        @pl.when(step > 0)
+                        def _():
+                            copy_res(which, index, col, place).wait()
+                    else:
+                        copy_res(which, index, col, place).wait()
+                    out[place] = dot_nn(lhs_t[slot], rhs[which, :, col * cols : (col + 1) * cols])
+                    turn(nxt, col)
+                    copy_res(which, index, col, place).start()
+                @pl.when(index + 2 < n_blk)
+                def _():
+                    copy_lhs(which, index + 2, slot).start()
+
+                if which == 0:
+
+                    @pl.when(index + 2 >= n_blk)
+                    def _():
+                        copy_lhs(1, index + 2 - n_blk, slot).start()
+            return carry
+
+        lax.fori_loop(0, n_blk // 2, pair, 0)
+
+    for slot in (0, 1):
+        for col in range(n_col):
+            copy_res(1, 0, col, slot * n_col + col).wait()
+
+
+def weight_grads(x, g, a, e):
+    rows, dim = x.shape
+    hid_dim = g.shape[1]
+    blk, cols = min(GRAD_ROWS, dim // 2), min(GRAD_COLS, hid_dim)
+    any_space = pl.BlockSpec(memory_space=pl.ANY)
+    dma = pltpu.SemaphoreType.DMA
+    n_col = hid_dim // cols
+    return pl.pallas_call(
+        functools.partial(grad_kernel, blk, cols),
+        out_shape=(jax.ShapeDtypeStruct((dim, hid_dim), F32), jax.ShapeDtypeStruct((hid_dim, dim), F32)),
+        in_specs=[any_space] * 4,
+        out_specs=(any_space, any_space),
+        scratch_shapes=[
+            pltpu.VMEM((2, rows, blk), BF16),
+            pltpu.VMEM((2, blk, rows), BF16),
+            pltpu.VMEM((2, rows, hid_dim), BF16),
+            pltpu.VMEM((2 * n_col, blk, cols), F32),
+            dma((2,)),
+            dma((2, n_col)),
+            dma((2 * n_col,)),
+        ],
+        compiler_params=pltpu.CompilerParams(vmem_limit_bytes=63 * 1024 * 1024),
+        name="grad_kernel",
+    )(x, g, a, e)
 
 
 def solution(mesh):
@@ -493,11 +611,7 @@
             w_out.reshape(hid_dim, model_dim),
         )
 
-        def over_rows(left, right):
-            return lax.dot_general(left, right, (((0,), (0,)), ((), ())), preferred_element_type=F32)
-
-        grad_in = over_rows(layer_in, layer_pre)
-        grad_out = over_rows(layer_act, layer_grad)
+        grad_in, grad_out = weight_grads(layer_in, layer_pre, layer_act, layer_grad)
         return grad_in[None, None], grad_out[None, None], loss[0, :1]
 
     return jax.shard_map(

time: 597 us -> 607 us (1.017)
  Pallas kernels: 558 us -> 605 us
  matrix products: 37 us -> 0 us
    pallas_call x0 -> x1, Pallas kernels: none -> 46.7 us  [weight_grads(): pl.pallas_call(functools.partial(grad_kernel, blk, cols), out_shape=(jax....]
    dot_general x2 -> x0, matrix products: 37 us -> none  [over_rows(): lax.dot_general(left, right, (((0,), (0,)), ((), ())), preferred_element_...]
where the time goes in v4:
time: 607 us
  Pallas kernels  605 us (100%)
    pallas_call x1, Pallas kernels, stage_step(): pl.pallas_call(kernel, out_shape=(jax.ShapeDtypeStruct((rows, model_dim),...  558 us
    pallas_call x1, Pallas kernels, weight_grads(): pl.pallas_call(functools.partial(grad_kernel, blk, cols), out_shape=(jax....  46.7 us

profile of v4, /device:TPU:0, one launch (start us, length us, event | category | flops | bytes accessed | tf_op | source)
XLA Modules:
  0.0 606.6 jit_solution(13760745167056674034)
XLA Ops:
  0.6 557.9 %stage_kernel.1 = (bf16[1536,2048]{1,0:T(8,128)(2,1)}, bf16[1536,2048]{1,0:T(8,128)(2,1)}, bf16[1536,2048]{1,0:T(8,128)(2,1)}, bf16[1536,2048]{1,0:T(8,128)(2,1)}, f32[8,128]{1,0:T(8,128)}) custom-call(bf16[24,64,2048]{2,1,0:T(8,128)(2,1)} %bitcast.9, bf16[24,64,2048]{2,1,0:T(8,128)(2,1)} %bitcast.10, bf16[2048,2048]{1,0:T(8,128)(2,1)} %bitcast.7, ...), custom_call_target="tpu_custom_call" | custom-call | tf_op jit(solution)/shard_map/stage_kernel/pallas_call | solution.py:570
  558.6 1.2 slice.3
  559.8 46.7 %grad_kernel.1 = (f32[2048,2048]{1,0:T(8,128)}, f32[2048,2048]{1,0:T(8,128)}) custom-call(bf16[1536,2048]{1,0:T(8,128)(2,1)} %get-tuple-element.10.x_hbm, bf16[1536,2048]{1,0:T(8,128)(2,1)} %get-tuple-element.11.g_hbm, bf16[1536,2048]{1,0:T(8,128)(2,1)} %get-tuple-element.12.a_hbm, bf16[1536,2048]{1,0:T(8,128)(2,1)} %get-tuple-element.13.e_hbm), custom_call_target="tpu_custom_call" | custom-call | tf_op jit(solution)/shard_map/grad_kernel/pallas_call | solution.py:533

commit v5 on v3

--- a/solution.py
+++ b/solution.py
@@ -18,8 +18,11 @@
 RECV_SLOTS = 8
 LAST_LEAD = 5
 PREV_LEAD = 16
-FIRST_IDLE = 11
+FIRST_IDLE = 12
 NEXT_IDLE = 7
+FORE_CHUNKS = 6
+RELAY_CHUNKS = 18
+RELAY_START = 0
 
 BF16 = jnp.bfloat16
 F32 = jnp.float32
@@ -45,17 +48,18 @@
 
 
 def stage_kernel(
-    n_stage, n_model, n_chunk, half_pieces, piece, hop, lead, idle, grad_scale,
+    n_stage, n_model, n_chunk, half_pieces, piece, hop, lead, idle, n_fore, n_relay, grad_scale,
     inputs_hbm, targets_hbm, w1_hbm, w2_hbm,
     x_out, e_out, a_out, g_out, loss_out,
     wts, acts, hid, send_buf, recv_buf, loss_acc, loss_in,
-    w_sem, in_sem, tgt_sem, sum_send, sum_recv, gat_send, gat_recv, over_send, back_send, back_recv, down_send, out_sem,
-    loss_send, loss_recv, spent_sem,
+    w_sem, in_sem, tgt_sem, sum_send, sum_recv, gat_send, gat_recv, over_send, back_send, take_recv, down_send, out_sem,
+    loss_send, loss_recv, spent_sem, rel_send, rel_over, rel_recv, rel_in, free_sem,
 ):
     pos = lax.axis_index("model")
     stage = lax.axis_index("stage")
     last_pos = n_model - 1
     last_stage = n_stage - 1
+    fore_stage = n_stage - 2
     slots = half_pieces
     total = n_chunk * half_pieces
     half = half_pieces * piece
@@ -85,6 +89,9 @@
     def copy_in(chunk):
         return pltpu.make_async_copy(inputs_hbm.at[chunk], acts.at[0, chunk], in_sem.at[chunk])
 
+    def grad_in(chunk):
+        return pltpu.make_async_copy(inputs_hbm.at[chunk], acts.at[1, chunk], rel_in.at[chunk])
+
     def copy_targets(side):
         cols = pl.ds(side * half, half)
         return pltpu.make_async_copy(targets_hbm.at[:, :, cols], acts.at[1, :, :, cols], tgt_sem)
@@ -203,7 +210,11 @@
         def _():
             chunk = fwd_chunk(turn)
             if part == 0:
-                copy_in(chunk).wait()
+
+                @pl.when((stage != fore_stage) | (chunk >= n_fore))
+                def _():
+                    copy_in(chunk).wait()
+
                 copy_out(0, chunk).start()
             for col in range(part * hid_part, (part + 1) * hid_part, hid_cols):
                 cols = pl.ds(col, hid_cols)
@@ -221,6 +232,11 @@
         def _():
             chunk = bwd_chunk(turn)
             if part == 0:
+
+                @pl.when((stage == fore_stage) & (chunk < n_relay))
+                def _():
+                    grad_in(chunk).wait()
+
                 copy_out(1, chunk).start()
                 copy_out(0, chunk).wait()
             for col in range(part * hid_part, (part + 1) * hid_part, hid_cols):
@@ -327,12 +343,22 @@
                 def _():
                     pl.semaphore_wait(spent_sem.at[side], 1)
 
-                @pl.when(bwd)
-                def _():
-                    remote(
-                        acts.at[0, chunk, :, cols], acts.at[1, chunk, :, cols], down_send.at[side, out],
-                        back_recv.at[side, index], {"stage": stage - 1},
-                    ).start()
+                @pl.when(bwd & (stage == 1) & (index == (n_relay - 1) * half_pieces))
+                def _():
+                    pl.semaphore_wait(free_sem.at[side], 1)
+
+                relayed = (stage == last_stage) & (chunk < n_relay)
+                there = acts.at[1, chunk, :, cols]
+
+                @pl.when(bwd & relayed)
+                def _():
+                    arrived = rel_recv.at[side, jnp.minimum(index, n_relay * half_pieces - 1)]
+                    remote(acts.at[0, chunk, :, cols], there, down_send.at[side, out], arrived, {"stage": 0}).start()
+
+                @pl.when(bwd & jnp.logical_not(relayed))
+                def _():
+                    arrived = take_recv.at[side, index]
+                    remote(acts.at[0, chunk, :, cols], there, down_send.at[side, out], arrived, {"stage": stage - 1}).start()
 
     def gather_step(side, step):
         rank = rank_of(side)
@@ -346,11 +372,14 @@
         here = acts.at[1, chunk, :, cols]
         hand_on = remote(here, here, gat_send.at[side, out], gat_recv.at[side, index], down(side))
 
-        @pl.when(old & (rank > 0))
+        early_one = (stage == fore_stage - 1) & (chunk < n_fore)
+        early_old = (stage == fore_stage - 1) & (fwd_chunk(turn - 1) < n_fore)
+
+        @pl.when(old & (rank > 0) & jnp.logical_not(early_old))
         def _():
             left(gat_send.at[side, out], any_piece)
 
-        @pl.when(old & (stage < last_stage))
+        @pl.when(old & (stage < last_stage) & (jnp.logical_not(early_old) | (rank == last_pos)))
         def _():
             left(over_send.at[side, out], any_piece)
 
@@ -358,34 +387,79 @@
             def _():
                 pl.semaphore_signal(spent_sem.at[side], inc=1, device_id={"stage": stage + 1}, device_id_type=MESH)
 
-        @pl.when(fwd & (rank < last_pos))
-        def _():
-            hand_on.wait_recv()
-
-        @pl.when(fwd & (rank > 0))
-        def _():
-            hand_on.start()
-
-        @pl.when(fwd & (stage < last_stage))
-        def _():
-            remote(here, acts.at[0, chunk, :, cols], over_send.at[side, out], in_sem.at[chunk], {"stage": stage + 1}).start()
-
-    def back_step(side, step):
+        @pl.when(fwd & jnp.logical_not(early_one))
+        def _():
+            @pl.when(rank < last_pos)
+            def _():
+                hand_on.wait_recv()
+
+            @pl.when(rank > 0)
+            def _():
+                hand_on.start()
+
+            @pl.when(stage < last_stage)
+            def _():
+                arrived = in_sem.at[chunk]
+                remote(here, acts.at[0, chunk, :, cols], over_send.at[side, out], arrived, {"stage": stage + 1}).start()
+
+        @pl.when(fwd & early_one & (rank == last_pos))
+        def _():
+            arrived = take_recv.at[side, jnp.minimum(total + index, total + n_fore * half_pieces - 1)]
+            remote(here, acts.at[0, chunk, :, cols], over_send.at[side, out], arrived, {"stage": stage + 1}).start()
+
+    def take_step(side, step):
         rank = rank_of(side)
         place = step + early - hop * (last_pos - rank)
         turn = turn_of(place)
-        bwd, old = is_bwd(turn), is_bwd(turn - 1)
+        bwd = is_bwd(turn)
+
+        def takes(turn):
+            back = is_bwd(turn) & (stage < last_stage) & ((stage < fore_stage) | (bwd_chunk(turn) >= n_relay))
+            return back | (is_fwd(turn) & (stage == fore_stage) & (fwd_chunk(turn) < n_fore))
+
         out = piece_of(place)
-        chunk = jnp.clip(bwd_chunk(turn), 0, n_chunk - 1)
-        index = chunk * half_pieces + out
+        chunk = any_chunk(turn, bwd)
+        is_back = bwd.astype(jnp.int32)
+        index = chunk * half_pieces + out + (1 - is_back) * total
+        here = acts.at[is_back, chunk, :, piece_at(side, out)]
+        arrived = take_recv.at[side, jnp.minimum(index, total + n_fore * half_pieces - 1)]
+        hand_on = remote(here, here, back_send.at[side, out], arrived, down(side))
+
+        @pl.when(takes(turn - 1) & (rank > 0))
+        def _():
+            left(back_send.at[side, out], any_piece)
+
+        @pl.when(takes(turn))
+        def _():
+            hand_on.wait_recv()
+
+            @pl.when(rank > 0)
+            def _():
+                hand_on.start()
+
+    def relay_step(side, step):
+        rank = rank_of(side)
+        place = step - (n_chunk + RELAY_START) * half_pieces - hop * (last_pos - rank)
+        turn = turn_of(place)
+        out = piece_of(place)
+        chunk = jnp.clip(turn, 0, n_relay - 1)
         here = acts.at[1, chunk, :, piece_at(side, out)]
-        hand_on = remote(here, here, back_send.at[side, out], back_recv.at[side, index], down(side))
-
-        @pl.when(old & (rank > 0) & (stage < last_stage))
-        def _():
-            left(back_send.at[side, out], any_piece)
-
-        @pl.when(bwd & (stage < last_stage))
+        arrived = rel_recv.at[side, chunk * half_pieces + out]
+        hand_on = remote(here, here, rel_send.at[side, out], arrived, down(side))
+
+        @pl.when((turn >= 1) & (turn <= n_relay))
+        def _():
+            @pl.when(rank > 0)
+            def _():
+                left(rel_send.at[side, out], any_piece)
+
+            left(rel_over.at[side, out], any_piece)
+
+            @pl.when((turn == n_relay) & (out == half_pieces - 1) & (rank == last_pos))
+            def _():
+                pl.semaphore_signal(free_sem.at[side], inc=1, device_id={"stage": 1}, device_id_type=MESH)
+
+        @pl.when((turn >= 0) & (turn < n_relay))
         def _():
             hand_on.wait_recv()
 
@@ -393,17 +467,25 @@
             def _():
                 hand_on.start()
 
+            remote(here, here, rel_over.at[side, out], rel_in.at[chunk], {"stage": fore_stage}).start()
+
     def loop_step(step, carry):
-        back_step(0, step)
-        back_step(1, step)
+        take_step(0, step)
+        take_step(1, step)
         for part in range(PARTS):
             first_product(step, part)
         sum_steps(step)
         gather_step(0, step)
         gather_step(1, step)
+
+        @pl.when((stage == 0) & (step >= n_chunk * half_pieces))
+        def _():
+            relay_step(0, step)
+            relay_step(1, step)
+
         return carry
 
-    lax.fori_loop(1 - PARTS, n_steps, loop_step, 0)
+    lax.fori_loop(jnp.where(stage == fore_stage, -early, 1 - PARTS), n_steps, loop_step, 0)
 
     for side, owner in ((0, last_pos), (1, 0)):
         owns = (stage == last_stage) & (pos == owner)
@@ -446,7 +528,10 @@
         grad_scale = 1.0 / (rows * model_dim)
         lead = [n_chunk] * (n_stage - 2) + [min(PREV_LEAD, n_chunk), min(LAST_LEAD, n_chunk)]
         idle = [FIRST_IDLE] + [NEXT_IDLE] * (n_stage - 3) + [0, 0]
-        kernel = functools.partial(stage_kernel, n_stage, n_model, n_chunk, half_pieces, piece, HOP_LAG, lead, idle, grad_scale)
+        n_fore, n_relay = min(FORE_CHUNKS, n_chunk - 1), min(RELAY_CHUNKS, n_chunk - 1)
+        kernel = functools.partial(
+            stage_kernel, n_stage, n_model, n_chunk, half_pieces, piece, HOP_LAG, lead, idle, n_fore, n_relay, grad_scale
+        )
         any_space = pl.BlockSpec(memory_space=pl.ANY)
         dma = pltpu.SemaphoreType.DMA
         layer_in, layer_grad, layer_act, layer_pre, loss = pl.pallas_call(
@@ -477,11 +562,16 @@
                 dma((2, n_chunk * half_pieces)),
                 dma((2, half_pieces)),
                 dma((2, half_pieces)),
-                dma((2, n_chunk * half_pieces)),
+                dma((2, (n_chunk + n_fore) * half_pieces)),
                 dma((2, half_pieces)),
                 dma((4, n_chunk)),
                 dma((n_stage * n_model,)),
                 dma((2,)),
+                pltpu.SemaphoreType.REGULAR((2,)),
+                dma((2, half_pieces)),
+                dma((2, half_pieces)),
+                dma((2, n_relay * half_pieces)),
+                dma((n_relay,)),
                 pltpu.SemaphoreType.REGULAR((2,)),
             ],
             compiler_params=pltpu.CompilerParams(collective_id=0, has_side_effects=True, vmem_limit_bytes=63 * 1024 * 1024),

time: 597 us -> 587 us (0.983)
  Pallas kernels: 558 us -> 548 us
    pallas_call x1, Pallas kernels: 558 us -> 548 us  [stage_step(): pl.pallas_call(kernel, out_shape=(jax.ShapeDtypeStruct((rows, model_dim),...]
where the time goes in v5:
time: 587 us
  Pallas kernels  548 us (93%)
  matrix products  36.9 us (6%)
    pallas_call x1, Pallas kernels, stage_step(): pl.pallas_call(kernel, out_shape=(jax.ShapeDtypeStruct((rows, model_dim),...  548 us
    dot_general x2, matrix products, over_rows(): lax.dot_general(left, right, (((0,), (0,)), ((), ())), preferred_element_...  36.9 us

profile of v5, /device:TPU:0, one launch (start us, length us, event | category | flops | bytes accessed | tf_op | source)
XLA Modules:
  0.0 587.0 jit_solution(7463354242100160656)
XLA Ops:
  0.6 548.3 %stage_kernel.1 = (bf16[1536,2048]{1,0:T(8,128)(2,1)}, bf16[1536,2048]{1,0:T(8,128)(2,1)}, bf16[1536,2048]{1,0:T(8,128)(2,1)}, bf16[1536,2048]{1,0:T(8,128)(2,1)}, f32[8,128]{1,0:T(8,128)}) custom-call(bf16[24,64,2048]{2,1,0:T(8,128)(2,1)} %bitcast.15, bf16[24,64,2048]{2,1,0:T(8,128)(2,1)} %bitcast.16, bf16[2048,2048]{1,0:T(8,128)(2,1)} %bitcast.13, ...), custom_call_target="tpu_custom_call" | custom-call | tf_op jit(solution)/shard_map/stage_kernel/pallas_call | solution.py:537
  548.9 1.2 slice.3
  550.1 0.0 copy-start
  550.1 0.0 copy-start.1
  550.1 20.9 %convolution_bitcast_fusion.1 = f32[1,1,2048,2048]{3,2,1,0:T(8,128)} fusion(bf16[1536,2048]{1,0:T(8,128)(2,1)} %get-tuple-element.8, bf16[1536,2048]{1,0:T(8,128)(2,1)} %get-tuple-element.9), kind=kOutput, calls=%fused_computation.1 | convolution fusion | flops 12884901888 | bytes 29360128 | tf_op jit(solution)/shard_map/dot_general | solution.py:587
  571.0 0.0 copy-done
  571.0 0.0 copy-done.1
  571.0 16.0 %convolution_bitcast_fusion = f32[1,1,2048,2048]{3,2,1,0:T(8,128)} fusion(bf16[1536,2048]{1,0:T(8,128)(2,1)S(1)} %copy-done.1, bf16[1536,2048]{1,0:T(8,128)(2,1)S(1)} %copy-done), kind=kOutput, calls=%fused_computation | convolution fusion | flops 12884901888 | bytes 29360128 | tf_op jit(solution)/shard_map/dot_general | solution.py:587
Async XLA Ops:
  550.1 20.9 %copy-start = (bf16[1536,2048]{1,0:T(8,128)(2,1)S(1)}, bf16[1536,2048]{1,0:T(8,128)(2,1)}, u32[]{:S(2)}) copy-start(bf16[1536,2048]{1,0:T(8,128)(2,1)} %get-tuple-element.11) | copy-start | bytes 18874372
  550.1 20.9 %copy-start.1 = (bf16[1536,2048]{1,0:T(8,128)(2,1)S(1)}, bf16[1536,2048]{1,0:T(8,128)(2,1)}, u32[]{:S(2)}) copy-start(bf16[1536,2048]{1,0:T(8,128)(2,1)} %get-tuple-element.10) | copy-start | bytes 18874372

commit v6 on v5

--- a/solution.py
+++ b/solution.py
@@ -24,6 +24,9 @@
 RELAY_CHUNKS = 18
 RELAY_START = 0
 
+SUM, BACK, GATHER, EARLY, TAKE, FWD, BWD = 256, 512, 1024, 2048, 4096, 8192, 16384
+MARGIN = 16
+
 BF16 = jnp.bfloat16
 F32 = jnp.float32
 MESH = pl.DeviceIdType.MESH
@@ -53,14 +56,14 @@
     x_out, e_out, a_out, g_out, loss_out,
     wts, acts, hid, send_buf, recv_buf, loss_acc, loss_in,
     w_sem, in_sem, tgt_sem, sum_send, sum_recv, gat_send, gat_recv, over_send, back_send, take_recv, down_send, out_sem,
-    loss_send, loss_recv, spent_sem, rel_send, rel_over, rel_recv, rel_in, free_sem,
+    loss_send, loss_recv, spent_sem, rel_send, rel_over, rel_recv, rel_in, free_sem, table,
 ):
     pos = lax.axis_index("model")
     stage = lax.axis_index("stage")
     last_pos = n_model - 1
     last_stage = n_stage - 1
     fore_stage = n_stage - 2
-    slots = half_pieces
+    bits = half_pieces.bit_length() - 1
     total = n_chunk * half_pieces
     half = half_pieces * piece
     hid_dim = wts.shape[2]
@@ -72,7 +75,7 @@
         n_lead = jnp.where(stage == at, lead[at], n_lead)
         n_idle = jnp.where(stage == at, idle[at], n_idle)
     turns = 2 * n_chunk + n_idle
-    n_steps = turns * half_pieces + jnp.where(stage == 0, max(1 - half_pieces, -hop), 6 * hop + slots)
+    n_steps = turns * half_pieces + jnp.where(stage == 0, 1 - hop, half_pieces + hop * last_pos + 1)
     early = half_pieces + 3 * hop
 
     barrier = pltpu.get_barrier_semaphore()
@@ -83,8 +86,12 @@
             def _():
                 pl.semaphore_signal(barrier, inc=1, device_id={"stage": to_stage, "model": to_pos}, device_id_type=MESH)
 
-    copy_w1 = pltpu.make_async_copy(w1_hbm, wts.at[0], w_sem.at[0])
-    copy_w2 = pltpu.make_async_copy(w2_hbm, wts.at[1], w_sem.at[1])
+    copy_w2 = pltpu.make_async_copy(w2_hbm, wts.at[1], w_sem.at[PARTS])
+
+    def copy_w1(part):
+        cols = pl.ds(part * hid_part, hid_part)
+        return pltpu.make_async_copy(w1_hbm.at[:, cols], wts.at[0, :, cols], w_sem.at[part])
+
 
     def copy_in(chunk):
         return pltpu.make_async_copy(inputs_hbm.at[chunk], acts.at[0, chunk], in_sem.at[chunk])
@@ -105,7 +112,8 @@
     def _():
         copy_in(0).start()
 
-    copy_w1.start()
+    for part in range(PARTS):
+        copy_w1(part).start()
     copy_w2.start()
 
     @pl.when(stage == 0)
@@ -137,45 +145,75 @@
 
         lax.fori_loop(0, count * count, one, 0)
 
-    loss_acc[...] = jnp.zeros_like(loss_acc)
-    copy_w1.wait()
-
-    @pl.when(stage > 0)
-    def _():
-        copy_w2.wait()
-        transpose_weights()
-
-    pl.semaphore_wait(barrier, n_stage * n_model - 1)
-
     n_mixed = 2 * (n_chunk - n_lead)
     n_after = 2 * n_chunk - n_lead
     n_first = n_lead + n_idle
 
+    def fill(entry, carry):
+        turn = entry - MARGIN
+        after = turn - n_first
+        pair = (after + 1024) // 2 - 512
+        odd = (after + 1024) % 2 == 1
+        mixed = (after >= 0) & (after < n_mixed)
+        leads = (turn >= 0) & (turn < n_lead)
+        fwd = leads | (mixed & odd)
+        bwd = (after >= 0) & (after < n_after) & jnp.logical_not(mixed & odd)
+        chunk = jnp.where(leads, turn, jnp.where(odd, n_lead + pair, pair))
+        chunk = jnp.where(bwd & (after >= n_mixed), after - (n_chunk - n_lead), chunk)
+        early_one = fwd & (stage == fore_stage - 1) & (chunk < n_fore)
+        back = bwd & (stage < last_stage) & ((stage < fore_stage) | (chunk >= n_relay))
+        take = back | (fwd & (stage == fore_stage) & (chunk < n_fore))
+        word = jnp.int32(0)
+        for flag, bit in (
+            (fwd | (bwd & (stage > 0)), SUM),
+            (bwd, BACK),
+            (fwd & jnp.logical_not(early_one), GATHER),
+            (early_one, EARLY),
+            (take, TAKE),
+            (fwd, FWD),
+            (bwd, BWD),
+        ):
+            word = word + jnp.where(flag, bit, 0)
+        table[entry] = word
+        return carry
+
+    lax.fori_loop(0, table.shape[0], fill, 0)
+    loss_acc[...] = jnp.zeros_like(loss_acc)
+    copy_w1(0).wait()
+
+    @pl.when(stage > 0)
+    def _():
+        for part in range(1, PARTS):
+            copy_w1(part).wait()
+        copy_w2.wait()
+        transpose_weights()
+
+    pl.semaphore_wait(barrier, n_stage * n_model - 1)
+
     def turn_of(place):
-        return lax.div(place + 64 * half_pieces, half_pieces) - 64
-
-    def is_fwd(turn):
-        after = turn - n_first
-        odd = lax.rem(after + 1024, 2) == 1
-        return ((turn >= 0) & (turn < n_lead)) | ((after >= 0) & (after < n_mixed) & odd)
-
-    def is_bwd(turn):
-        after = turn - n_first
-        odd = lax.rem(after + 1024, 2) == 1
-        return (after >= 0) & (after < n_after) & jnp.logical_not((after < n_mixed) & odd)
+        return lax.shift_right_logical(place + MARGIN * half_pieces, jnp.int32(bits))
+
+    def piece_of(place):
+        return lax.bitwise_and(place + MARGIN * half_pieces, jnp.int32(half_pieces - 1))
+
+    def has(word, mask):
+        return lax.bitwise_and(word, jnp.int32(mask)) != 0
 
     def fwd_chunk(turn):
-        return jnp.where(turn < n_lead, turn, n_lead + lax.div(turn - n_first + 1024, 2) - 512)
+        after = turn - (n_first + MARGIN)
+        return jnp.where(turn < n_lead + MARGIN, turn - MARGIN, n_lead + lax.shift_right_arithmetic(after, jnp.int32(1)))
 
     def bwd_chunk(turn):
-        after = turn - n_first
-        return jnp.where(after < n_mixed, lax.div(after + 1024, 2) - 512, after - (n_chunk - n_lead))
-
-    def piece_of(place):
-        return lax.rem(place + 64 * half_pieces, half_pieces)
-
-    def any_chunk(turn, bwd):
-        return jnp.clip(jnp.where(bwd, bwd_chunk(turn), fwd_chunk(turn)), 0, n_chunk - 1)
+        after = turn - (n_first + MARGIN)
+        return jnp.where(after < n_mixed, lax.shift_right_arithmetic(after, jnp.int32(1)), after - (n_chunk - n_lead))
+
+    def back_of(turn):
+        after = turn - (n_first + MARGIN)
+        odd = lax.bitwise_and(after, jnp.int32(1)) == 1
+        return ((after >= 0) & jnp.logical_not((after < n_mixed) & odd)).astype(jnp.int32)
+
+    def chunk_of(turn, is_back):
+        return jnp.clip(jnp.where(is_back == 1, bwd_chunk(turn), fwd_chunk(turn)), 0, n_chunk - 1)
 
     def piece_at(side, index):
         col = side * half + index * piece
@@ -189,8 +227,8 @@
     def left(send_sem, like):
         remote(like, like, send_sem, loss_recv.at[0], {"model": pos}).wait_send()
 
-    any_piece = acts.at[0, 0, :, pl.ds(0, piece)]
-    any_sum = send_buf.at[0, 0]
+    turn_pieces = acts.at[0, 0, :, pl.ds(0, half)]
+    turn_sums = send_buf.at[0, 0]
 
     def rank_of(side):
         return pos if side == 0 else last_pos - pos
@@ -204,9 +242,10 @@
     def first_product(step, part):
         place = step + PARTS - 1 - part
         turn = turn_of(place)
+        word = table[turn]
         starts = piece_of(place) == 0
 
-        @pl.when(starts & is_fwd(turn))
+        @pl.when(starts & has(word, FWD))
         def _():
             chunk = fwd_chunk(turn)
             if part == 0:
@@ -216,6 +255,12 @@
                     copy_in(chunk).wait()
 
                 copy_out(0, chunk).start()
+            else:
+
+                @pl.when((stage == 0) & (place == 0))
+                def _():
+                    copy_w1(part).wait()
+
             for col in range(part * hid_part, (part + 1) * hid_part, hid_cols):
                 cols = pl.ds(col, hid_cols)
                 pre = dot_nn(acts[0, chunk], wts[0, :, cols]).astype(BF16)
@@ -224,11 +269,11 @@
             if part == PARTS - 1:
                 copy_out(2, chunk).start()
 
-                @pl.when((stage == 0) & (turn == 0))
+                @pl.when((stage == 0) & (place == 0))
                 def _():
                     copy_w2.wait()
 
-        @pl.when(starts & is_bwd(turn))
+        @pl.when(starts & has(word, BWD))
         def _():
             chunk = bwd_chunk(turn)
             if part == 0:
@@ -274,39 +319,42 @@
             rank = rank_of(side)
             place = step - hop * rank
             turn = turn_of(place)
-            fwd, bwd = is_fwd(turn), is_bwd(turn)
-            old_fwd, old_bwd = is_fwd(turn - 1), is_bwd(turn - 1)
-            out = piece_of(place)
-            inn = lax.rem(place + 64 * RECV_SLOTS, RECV_SLOTS)
-            is_back = bwd.astype(jnp.int32)
-            sums = fwd | (bwd & (stage > 0))
-            now.append((rank, fwd, bwd, sums, is_back, any_chunk(turn, bwd), out, inn, piece_at(side, out)))
-
-            @pl.when((old_fwd | (old_bwd & (stage > 0))) & (rank < last_pos))
-            def _():
-                left(sum_send.at[side, out], any_sum)
-
-            @pl.when(old_bwd & (stage > 0) & (rank == last_pos))
-            def _():
-                left(down_send.at[side, out], any_piece)
-
-        @pl.when(now[0][3] | now[1][3])
+            word, old = table[turn], table[turn - 2]
+            index = piece_of(place)
+            half_turn = lax.bitwise_and(turn, jnp.int32(1))
+            inn = lax.bitwise_and(place + MARGIN * half_pieces, jnp.int32(RECV_SLOTS - 1))
+            sums = has(word, SUM)
+            is_back = back_of(turn)
+            now.append((rank, word, sums, is_back, chunk_of(turn, is_back), index, half_turn, inn, piece_at(side, index)))
+
+            @pl.when((index == 0) & has(old, SUM))
+            def _():
+                @pl.when(rank < last_pos)
+                def _():
+                    left(sum_send.at[side, half_turn], turn_sums)
+
+                @pl.when((rank == last_pos) & has(old, BACK))
+                def _():
+                    left(down_send.at[side, half_turn], turn_pieces)
+
+        @pl.when(now[0][2] | now[1][2])
         def _():
             for side in (0, 1):
-                _, _, _, _, is_back, chunk, out, _, cols = now[side]
-                send_buf[side, out] = dot_nn(hid[is_back, chunk], wts[1 + 2 * is_back, :, cols])
+                _, _, _, is_back, chunk, index, half_turn, _, cols = now[side]
+                send_buf[side, half_turn, index] = dot_nn(hid[is_back, chunk], wts[1 + 2 * is_back, :, cols])
 
         for side in (0, 1):
-            rank, fwd, bwd, sums, is_back, chunk, out, inn, cols = now[side]
+            rank, word, sums, is_back, chunk, out, half_turn, inn, cols = now[side]
+            bwd = has(word, BACK)
             index = chunk * half_pieces + out
-            hand_on = remote(
-                send_buf.at[side, out], recv_buf.at[side, inn], sum_send.at[side, out], sum_recv.at[side, inn], up(side)
-            )
+            mine = send_buf.at[side, half_turn, out]
+            gone = down_send.at[side, half_turn]
+            hand_on = remote(mine, recv_buf.at[side, inn], sum_send.at[side, half_turn], sum_recv.at[side, inn], up(side))
 
             @pl.when(sums & (rank > 0))
             def _():
                 hand_on.wait_recv()
-                send_buf[side, out] = send_buf[side, out] + recv_buf[side, inn]
+                mine[...] = mine[...] + recv_buf[side, inn]
 
             @pl.when(sums & (rank < last_pos))
             def _():
@@ -314,8 +362,8 @@
 
             @pl.when(sums & (rank == last_pos))
             def _():
-                whole = acts[is_back, chunk, :, cols].astype(F32) + send_buf[side, out]
-                scored = fwd & (stage == last_stage)
+                whole = acts[is_back, chunk, :, cols].astype(F32) + mine[...]
+                scored = has(word, FWD) & (stage == last_stage)
 
                 @pl.when(scored)
                 def _():
@@ -339,11 +387,11 @@
                 def _():
                     acts[1 - is_back, chunk, :, cols] = whole.astype(BF16)
 
-                @pl.when(bwd & (index == total - half_pieces))
+                @pl.when(bwd & (index == total - 2 * half_pieces))
                 def _():
                     pl.semaphore_wait(spent_sem.at[side], 1)
 
-                @pl.when(bwd & (stage == 1) & (index == (n_relay - 1) * half_pieces))
+                @pl.when(bwd & (stage == 1) & (index == (n_relay - 2) * half_pieces))
                 def _():
                     pl.semaphore_wait(free_sem.at[side], 1)
 
@@ -353,42 +401,44 @@
                 @pl.when(bwd & relayed)
                 def _():
                     arrived = rel_recv.at[side, jnp.minimum(index, n_relay * half_pieces - 1)]
-                    remote(acts.at[0, chunk, :, cols], there, down_send.at[side, out], arrived, {"stage": 0}).start()
+                    remote(acts.at[0, chunk, :, cols], there, gone, arrived, {"stage": 0}).start()
 
                 @pl.when(bwd & jnp.logical_not(relayed))
                 def _():
                     arrived = take_recv.at[side, index]
-                    remote(acts.at[0, chunk, :, cols], there, down_send.at[side, out], arrived, {"stage": stage - 1}).start()
+                    remote(acts.at[0, chunk, :, cols], there, gone, arrived, {"stage": stage - 1}).start()
 
     def gather_step(side, step):
         rank = rank_of(side)
         place = step - 3 * hop - hop * (last_pos - rank)
         turn = turn_of(place)
-        fwd, old = is_fwd(turn), is_fwd(turn - 1)
+        word, old = table[turn], table[turn - 2]
         out = piece_of(place)
+        half_turn = lax.bitwise_and(turn, jnp.int32(1))
         chunk = jnp.clip(fwd_chunk(turn), 0, n_chunk - 1)
         index = chunk * half_pieces + out
         cols = piece_at(side, out)
         here = acts.at[1, chunk, :, cols]
-        hand_on = remote(here, here, gat_send.at[side, out], gat_recv.at[side, index], down(side))
-
-        early_one = (stage == fore_stage - 1) & (chunk < n_fore)
-        early_old = (stage == fore_stage - 1) & (fwd_chunk(turn - 1) < n_fore)
-
-        @pl.when(old & (rank > 0) & jnp.logical_not(early_old))
-        def _():
-            left(gat_send.at[side, out], any_piece)
-
-        @pl.when(old & (stage < last_stage) & (jnp.logical_not(early_old) | (rank == last_pos)))
-        def _():
-            left(over_send.at[side, out], any_piece)
-
-            @pl.when((fwd_chunk(turn - 1) == n_chunk - 1) & (out == half_pieces - 1) & (rank == last_pos))
-            def _():
-                pl.semaphore_signal(spent_sem.at[side], inc=1, device_id={"stage": stage + 1}, device_id_type=MESH)
-
-        @pl.when(fwd & jnp.logical_not(early_one))
-        def _():
+        gone = over_send.at[side, half_turn]
+
+        @pl.when((out == 0) & has(old, GATHER | EARLY))
+        def _():
+            @pl.when(has(old, GATHER) & (rank > 0))
+            def _():
+                left(gat_send.at[side, half_turn], turn_pieces)
+
+            @pl.when((stage < last_stage) & (has(old, GATHER) | (rank == last_pos)))
+            def _():
+                left(gone, turn_pieces)
+
+                @pl.when((fwd_chunk(turn - 2) == n_chunk - 1) & (rank == last_pos))
+                def _():
+                    pl.semaphore_signal(spent_sem.at[side], inc=1, device_id={"stage": stage + 1}, device_id_type=MESH)
+
+        @pl.when(has(word, GATHER))
+        def _():
+            hand_on = remote(here, here, gat_send.at[side, half_turn], gat_recv.at[side, index], down(side))
+
             @pl.when(rank < last_pos)
             def _():
                 hand_on.wait_recv()
@@ -399,38 +449,32 @@
 
             @pl.when(stage < last_stage)
             def _():
-                arrived = in_sem.at[chunk]
-                remote(here, acts.at[0, chunk, :, cols], over_send.at[side, out], arrived, {"stage": stage + 1}).start()
-
-        @pl.when(fwd & early_one & (rank == last_pos))
+                remote(here, acts.at[0, chunk, :, cols], gone, in_sem.at[chunk], {"stage": stage + 1}).start()
+
+        @pl.when(has(word, EARLY) & (rank == last_pos))
         def _():
             arrived = take_recv.at[side, jnp.minimum(total + index, total + n_fore * half_pieces - 1)]
-            remote(here, acts.at[0, chunk, :, cols], over_send.at[side, out], arrived, {"stage": stage + 1}).start()
+            remote(here, acts.at[0, chunk, :, cols], gone, arrived, {"stage": stage + 1}).start()
 
     def take_step(side, step):
         rank = rank_of(side)
         place = step + early - hop * (last_pos - rank)
         turn = turn_of(place)
-        bwd = is_bwd(turn)
-
-        def takes(turn):
-            back = is_bwd(turn) & (stage < last_stage) & ((stage < fore_stage) | (bwd_chunk(turn) >= n_relay))
-            return back | (is_fwd(turn) & (stage == fore_stage) & (fwd_chunk(turn) < n_fore))
-
+        word, old = table[turn], table[turn - 2]
         out = piece_of(place)
-        chunk = any_chunk(turn, bwd)
-        is_back = bwd.astype(jnp.int32)
-        index = chunk * half_pieces + out + (1 - is_back) * total
-        here = acts.at[is_back, chunk, :, piece_at(side, out)]
-        arrived = take_recv.at[side, jnp.minimum(index, total + n_fore * half_pieces - 1)]
-        hand_on = remote(here, here, back_send.at[side, out], arrived, down(side))
-
-        @pl.when(takes(turn - 1) & (rank > 0))
-        def _():
-            left(back_send.at[side, out], any_piece)
-
-        @pl.when(takes(turn))
-        def _():
+        gone = back_send.at[side, lax.bitwise_and(turn, jnp.int32(1))]
+
+        @pl.when((out == 0) & has(old, TAKE) & (rank > 0))
+        def _():
+            left(gone, turn_pieces)
+
+        @pl.when(has(word, TAKE))
+        def _():
+            is_back = back_of(turn)
+            chunk = chunk_of(turn, is_back)
+            index = chunk * half_pieces + out + (1 - is_back) * total
+            here = acts.at[is_back, chunk, :, piece_at(side, out)]
+            hand_on = remote(here, here, gone, take_recv.at[side, index], down(side))
             hand_on.wait_recv()
 
             @pl.when(rank > 0)
@@ -440,22 +484,23 @@
     def relay_step(side, step):
         rank = rank_of(side)
         place = step - (n_chunk + RELAY_START) * half_pieces - hop * (last_pos - rank)
-        turn = turn_of(place)
+        turn = turn_of(place) - MARGIN
         out = piece_of(place)
+        half_turn = lax.bitwise_and(turn, jnp.int32(1))
         chunk = jnp.clip(turn, 0, n_relay - 1)
         here = acts.at[1, chunk, :, piece_at(side, out)]
-        arrived = rel_recv.at[side, chunk * half_pieces + out]
-        hand_on = remote(here, here, rel_send.at[side, out], arrived, down(side))
-
-        @pl.when((turn >= 1) & (turn <= n_relay))
+        gone = rel_over.at[side, half_turn]
+        hand_on = remote(here, here, rel_send.at[side, half_turn], rel_recv.at[side, chunk * half_pieces + out], down(side))
+
+        @pl.when((out == 0) & (turn >= 2) & (turn < n_relay + 2))
         def _():
             @pl.when(rank > 0)
             def _():
-                left(rel_send.at[side, out], any_piece)
-
-            left(rel_over.at[side, out], any_piece)
-
-            @pl.when((turn == n_relay) & (out == half_pieces - 1) & (rank == last_pos))
+                left(rel_send.at[side, half_turn], turn_pieces)
+
+            left(gone, turn_pieces)
+
+            @pl.when((turn == n_relay + 1) & (rank == last_pos))
             def _():
                 pl.semaphore_signal(free_sem.at[side], inc=1, device_id={"stage": 1}, device_id_type=MESH)
 
@@ -467,7 +512,7 @@
             def _():
                 hand_on.start()
 
-            remote(here, here, rel_over.at[side, out], rel_in.at[chunk], {"stage": fore_stage}).start()
+            remote(here, here, gone, rel_in.at[chunk], {"stage": fore_stage}).start()
 
     def loop_step(step, carry):
         take_step(0, step)
@@ -549,30 +594,31 @@
                 pltpu.VMEM((4, model_dim, hid_dim), BF16),
                 pltpu.VMEM((2, n_chunk, chunk, model_dim), BF16),
                 pltpu.VMEM((2, n_chunk, chunk, hid_dim), BF16),
-                pltpu.VMEM((2, half_pieces, chunk, piece), F32),
+                pltpu.VMEM((2, 2, half_pieces, chunk, piece), F32),
                 pltpu.VMEM((2, RECV_SLOTS, chunk, piece), F32),
                 pltpu.VMEM((8, 128), F32),
                 pltpu.VMEM((2, 8, 128), F32),
-                dma((2,)),
+                dma((PARTS + 1,)),
                 dma((n_chunk,)),
                 dma,
-                dma((2, half_pieces)),
+                dma((2, 2)),
                 dma((2, RECV_SLOTS)),
-                dma((2, half_pieces)),
+                dma((2, 2)),
                 dma((2, n_chunk * half_pieces)),
-                dma((2, half_pieces)),
-                dma((2, half_pieces)),
+                dma((2, 2)),
+                dma((2, 2)),
                 dma((2, (n_chunk + n_fore) * half_pieces)),
-                dma((2, half_pieces)),
+                dma((2, 2)),
                 dma((4, n_chunk)),
                 dma((n_stage * n_model,)),
                 dma((2,)),
                 pltpu.SemaphoreType.REGULAR((2,)),
-                dma((2, half_pieces)),
-                dma((2, half_pieces)),
+                dma((2, 2)),
+                dma((2, 2)),
                 dma((2, n_relay * half_pieces)),
                 dma((n_relay,)),
                 pltpu.SemaphoreType.REGULAR((2,)),
+                pltpu.SMEM((2 * n_chunk + max(idle) + 2 * MARGIN,), jnp.int32),
             ],
             compiler_params=pltpu.CompilerParams(collective_id=0, has_side_effects=True, vmem_limit_bytes=63 * 1024 * 1024),
             name="stage_kernel",

time: 587 us -> 583 us (level)
  no operation moved by 1% of the time
where the time goes in v6:
time: 583 us; the launch traced here: 582 us
  Pallas kernels  543 us (93%)
  matrix products  36.9 us (6%)
    pallas_call x1, Pallas kernels, stage_step(): pl.pallas_call(kernel, out_shape=(jax.ShapeDtypeStruct((rows, model_dim),...  543 us
    dot_general x2, matrix products, over_rows(): lax.dot_general(left, right, (((0,), (0,)), ((), ())), preferred_element_...  36.9 us

profile of v6, /device:TPU:0, one launch (start us, length us, event | category | flops | bytes accessed | tf_op | source)
XLA Modules:
  0.0 581.6 jit_solution(10026389505205481556)
XLA Ops:
  0.6 542.9 %stage_kernel.1 = (bf16[1536,2048]{1,0:T(8,128)(2,1)}, bf16[1536,2048]{1,0:T(8,128)(2,1)}, bf16[1536,2048]{1,0:T(8,128)(2,1)}, bf16[1536,2048]{1,0:T(8,128)(2,1)}, f32[8,128]{1,0:T(8,128)}) custom-call(bf16[24,64,2048]{2,1,0:T(8,128)(2,1)} %bitcast.15, bf16[24,64,2048]{2,1,0:T(8,128)(2,1)} %bitcast.16, bf16[2048,2048]{1,0:T(8,128)(2,1)} %bitcast.13, ...), custom_call_target="tpu_custom_call" | custom-call | tf_op jit(solution)/shard_map/stage_kernel/pallas_call | solution.py:582
  543.6 1.2 slice.3
  544.7 0.0 copy-start
  544.7 0.0 copy-start.1
  544.7 20.9 %convolution_bitcast_fusion.1 = f32[1,1,2048,2048]{3,2,1,0:T(8,128)} fusion(bf16[1536,2048]{1,0:T(8,128)(2,1)} %get-tuple-element.8, bf16[1536,2048]{1,0:T(8,128)(2,1)} %get-tuple-element.9), kind=kOutput, calls=%fused_computation.1 | convolution fusion | flops 12884901888 | bytes 29360128 | tf_op jit(solution)/shard_map/dot_general | solution.py:633
  565.6 0.0 copy-done
  565.6 0.0 copy-done.1
  565.6 16.0 %convolution_bitcast_fusion = f32[1,1,2048,2048]{3,2,1,0:T(8,128)} fusion(bf16[1536,2048]{1,0:T(8,128)(2,1)S(1)} %copy-done.1, bf16[1536,2048]{1,0:T(8,128)(2,1)S(1)} %copy-done), kind=kOutput, calls=%fused_computation | convolution fusion | flops 12884901888 | bytes 29360128 | tf_op jit(solution)/shard_map/dot_general | solution.py:633
Async XLA Ops:
  544.7 20.9 %copy-start = (bf16[1536,2048]{1,0:T(8,128)(2,1)S(1)}, bf16[1536,2048]{1,0:T(8,128)(2,1)}, u32[]{:S(2)}) copy-start(bf16[1536,2048]{1,0:T(8,128)(2,1)} %get-tuple-element.11) | copy-start | bytes 18874372
  544.7 20.9 %copy-start.1 = (bf16[1536,2048]{1,0:T(8,128)(2,1)S(1)}, bf16[1536,2048]{1,0:T(8,128)(2,1)}, u32[]{:S(2)}) copy-start(bf16[1536,2048]{1,0:T(8,128)(2,1)} %get-tuple-element.10) | copy-start | bytes 18874372

commit v7 on v6

--- a/solution.py
+++ b/solution.py
@@ -25,7 +25,7 @@
 RELAY_START = 0
 
 SUM, BACK, GATHER, EARLY, TAKE, FWD, BWD = 256, 512, 1024, 2048, 4096, 8192, 16384
-MARGIN = 16
+MARGIN = 8
 
 BF16 = jnp.bfloat16
 F32 = jnp.float32
@@ -76,7 +76,7 @@
         n_idle = jnp.where(stage == at, idle[at], n_idle)
     turns = 2 * n_chunk + n_idle
     n_steps = turns * half_pieces + jnp.where(stage == 0, 1 - hop, half_pieces + hop * last_pos + 1)
-    early = half_pieces + 3 * hop
+    early = half_pieces + 3 * hop + 1
 
     barrier = pltpu.get_barrier_semaphore()
     for to_stage in range(n_stage):
@@ -515,19 +515,19 @@
             remote(here, here, gone, rel_in.at[chunk], {"stage": fore_stage}).start()
 
     def loop_step(step, carry):
-        take_step(0, step)
-        take_step(1, step)
         for part in range(PARTS):
             first_product(step, part)
         sum_steps(step)
+        take_step(0, step)
+        take_step(1, step)
+
+        @pl.when((stage == 0) & (step >= n_chunk * half_pieces))
+        def _():
+            relay_step(0, step)
+            relay_step(1, step)
+
         gather_step(0, step)
         gather_step(1, step)
-
-        @pl.when((stage == 0) & (step >= n_chunk * half_pieces))
-        def _():
-            relay_step(0, step)
-            relay_step(1, step)
-
         return carry
 
     lax.fori_loop(jnp.where(stage == fore_stage, -early, 1 - PARTS), n_steps, loop_step, 0)

time: 583 us -> 581 us (level)
  no operation moved by 1% of the time
where the time goes in v7:
time: 581 us
  Pallas kernels  542 us (93%)
  matrix products  36.9 us (6%)
    pallas_call x1, Pallas kernels, stage_step(): pl.pallas_call(kernel, out_shape=(jax.ShapeDtypeStruct((rows, model_dim),...  542 us
    dot_general x2, matrix products, over_rows(): lax.dot_general(left, right, (((0,), (0,)), ((), ())), preferred_element_...  36.9 us

profile of v7, /device:TPU:0, one launch (start us, length us, event | category | flops | bytes accessed | tf_op | source)
XLA Modules:
  0.0 581.2 jit_solution(2178455080522387000)
XLA Ops:
  0.6 542.5 %stage_kernel.1 = (bf16[1536,2048]{1,0:T(8,128)(2,1)}, bf16[1536,2048]{1,0:T(8,128)(2,1)}, bf16[1536,2048]{1,0:T(8,128)(2,1)}, bf16[1536,2048]{1,0:T(8,128)(2,1)}, f32[8,128]{1,0:T(8,128)}) custom-call(bf16[24,64,2048]{2,1,0:T(8,128)(2,1)} %bitcast.15, bf16[24,64,2048]{2,1,0:T(8,128)(2,1)} %bitcast.16, bf16[2048,2048]{1,0:T(8,128)(2,1)} %bitcast.13, ...), custom_call_target="tpu_custom_call" | custom-call | tf_op jit(solution)/shard_map/stage_kernel/pallas_call | solution.py:582
  543.1 1.2 slice.3
  544.3 0.0 copy-start
  544.3 0.0 copy-start.1
  544.3 20.9 %convolution_bitcast_fusion.1 = f32[1,1,2048,2048]{3,2,1,0:T(8,128)} fusion(bf16[1536,2048]{1,0:T(8,128)(2,1)} %get-tuple-element.8, bf16[1536,2048]{1,0:T(8,128)(2,1)} %get-tuple-element.9), kind=kOutput, calls=%fused_computation.1 | convolution fusion | flops 12884901888 | bytes 29360128 | tf_op jit(solution)/shard_map/dot_general | solution.py:633
  565.2 0.0 copy-done
  565.2 0.0 copy-done.1
  565.2 16.0 %convolution_bitcast_fusion = f32[1,1,2048,2048]{3,2,1,0:T(8,128)} fusion(bf16[1536,2048]{1,0:T(8,128)(2,1)S(1)} %copy-done.1, bf16[1536,2048]{1,0:T(8,128)(2,1)S(1)} %copy-done), kind=kOutput, calls=%fused_computation | convolution fusion | flops 12884901888 | bytes 29360128 | tf_op jit(solution)/shard_map/dot_general | solution.py:633
Async XLA Ops:
  544.3 20.9 %copy-start = (bf16[1536,2048]{1,0:T(8,128)(2,1)S(1)}, bf16[1536,2048]{1,0:T(8,128)(2,1)}, u32[]{:S(2)}) copy-start(bf16[1536,2048]{1,0:T(8,128)(2,1)} %get-tuple-element.11) | copy-start | bytes 18874372
  544.3 20.9 %copy-start.1 = (bf16[1536,2048]{1,0:T(8,128)(2,1)S(1)}, bf16[1536,2048]{1,0:T(8,128)(2,1)}, u32[]{:S(2)}) copy-start(bf16[1536,2048]{1,0:T(8,128)(2,1)} %get-tuple-element.10) | copy-start | bytes 18874372

commit v8 on v7

--- a/solution.py
+++ b/solution.py
@@ -188,7 +188,13 @@
         copy_w2.wait()
         transpose_weights()
 
-    pl.semaphore_wait(barrier, n_stage * n_model - 1)
+    def meet():
+        pl.semaphore_wait(barrier, n_stage * n_model - 1)
+
+    @pl.when(stage == fore_stage)
+    def _():
+        meet()
+
 
     def turn_of(place):
         return lax.shift_right_logical(place + MARGIN * half_pieces, jnp.int32(bits))
@@ -410,7 +416,7 @@
 
     def gather_step(side, step):
         rank = rank_of(side)
-        place = step - 3 * hop - hop * (last_pos - rank)
+        place = step - 1 - 3 * hop - hop * (last_pos - rank)
         turn = turn_of(place)
         word, old = table[turn], table[turn - 2]
         out = piece_of(place)
@@ -517,17 +523,22 @@
     def loop_step(step, carry):
         for part in range(PARTS):
             first_product(step, part)
+
+        @pl.when((step == 0) & (stage != fore_stage))
+        def _():
+            meet()
+
+        gather_step(0, step)
+        gather_step(1, step)
         sum_steps(step)
+
+        @pl.when((stage == 0) & (step >= n_chunk * half_pieces))
+        def _():
+            relay_step(0, step)
+            relay_step(1, step)
+
         take_step(0, step)
         take_step(1, step)
-
-        @pl.when((stage == 0) & (step >= n_chunk * half_pieces))
-        def _():
-            relay_step(0, step)
-            relay_step(1, step)
-
-        gather_step(0, step)
-        gather_step(1, step)
         return carry
 
     lax.fori_loop(jnp.where(stage == fore_stage, -early, 1 - PARTS), n_steps, loop_step, 0)

time: 581 us -> 578 us (level)
  no operation moved by 1% of the time
where the time goes in v8:
time: 578 us
  Pallas kernels  539 us (93%)
  matrix products  36.9 us (6%)
    pallas_call x1, Pallas kernels, stage_step(): pl.pallas_call(kernel, out_shape=(jax.ShapeDtypeStruct((rows, model_dim),...  539 us
    dot_general x2, matrix products, over_rows(): lax.dot_general(left, right, (((0,), (0,)), ((), ())), preferred_element_...  36.9 us

profile of v8, /device:TPU:0, one launch (start us, length us, event | category | flops | bytes accessed | tf_op | source)
XLA Modules:
  0.0 578.1 jit_solution(2535831400100808139)
XLA Ops:
  0.6 539.3 %stage_kernel.1 = (bf16[1536,2048]{1,0:T(8,128)(2,1)}, bf16[1536,2048]{1,0:T(8,128)(2,1)}, bf16[1536,2048]{1,0:T(8,128)(2,1)}, bf16[1536,2048]{1,0:T(8,128)(2,1)}, f32[8,128]{1,0:T(8,128)}) custom-call(bf16[24,64,2048]{2,1,0:T(8,128)(2,1)} %bitcast.15, bf16[24,64,2048]{2,1,0:T(8,128)(2,1)} %bitcast.16, bf16[2048,2048]{1,0:T(8,128)(2,1)} %bitcast.13, ...), custom_call_target="tpu_custom_call" | custom-call | tf_op jit(solution)/shard_map/stage_kernel/pallas_call | solution.py:593
  540.0 1.2 slice.3
  541.2 0.0 copy-start
  541.2 0.0 copy-start.1
  541.2 20.9 %convolution_bitcast_fusion.1 = f32[1,1,2048,2048]{3,2,1,0:T(8,128)} fusion(bf16[1536,2048]{1,0:T(8,128)(2,1)} %get-tuple-element.8, bf16[1536,2048]{1,0:T(8,128)(2,1)} %get-tuple-element.9), kind=kOutput, calls=%fused_computation.1 | convolution fusion | flops 12884901888 | bytes 29360128 | tf_op jit(solution)/shard_map/dot_general | solution.py:644
  562.0 0.0 copy-done
  562.1 0.0 copy-done.1
  562.1 16.0 %convolution_bitcast_fusion = f32[1,1,2048,2048]{3,2,1,0:T(8,128)} fusion(bf16[1536,2048]{1,0:T(8,128)(2,1)S(1)} %copy-done.1, bf16[1536,2048]{1,0:T(8,128)(2,1)S(1)} %copy-done), kind=kOutput, calls=%fused_computation | convolution fusion | flops 12884901888 | bytes 29360128 | tf_op jit(solution)/shard_map/dot_general | solution.py:644
Async XLA Ops:
  541.2 20.9 %copy-start = (bf16[1536,2048]{1,0:T(8,128)(2,1)S(1)}, bf16[1536,2048]{1,0:T(8,128)(2,1)}, u32[]{:S(2)}) copy-start(bf16[1536,2048]{1,0:T(8,128)(2,1)} %get-tuple-element.11) | copy-start | bytes 18874372
  541.2 20.9 %copy-start.1 = (bf16[1536,2048]{1,0:T(8,128)(2,1)S(1)}, bf16[1536,2048]{1,0:T(8,128)(2,1)}, u32[]{:S(2)}) copy-start(bf16[1536,2048]{1,0:T(8,128)(2,1)} %get-tuple-element.10) | copy-start | bytes 18874372

commit v9 on v8

--- a/solution.py
+++ b/solution.py
@@ -24,6 +24,11 @@
 RELAY_CHUNKS = 18
 RELAY_START = 0
 
+FIRST_GRADS = 12
+TILE_ROWS = 256
+TILE_COLS = 1024
+TILE_STEPS = 2
+
 SUM, BACK, GATHER, EARLY, TAKE, FWD, BWD = 256, 512, 1024, 2048, 4096, 8192, 16384
 MARGIN = 8
 
@@ -51,12 +56,12 @@
 
 
 def stage_kernel(
-    n_stage, n_model, n_chunk, half_pieces, piece, hop, lead, idle, n_fore, n_relay, grad_scale,
+    n_stage, n_model, n_chunk, half_pieces, piece, hop, lead, idle, n_fore, n_relay, n_grad, grad_scale,
     inputs_hbm, targets_hbm, w1_hbm, w2_hbm,
-    x_out, e_out, a_out, g_out, loss_out,
+    x_out, e_out, a_out, g_out, grad_hbm, loss_out,
     wts, acts, hid, send_buf, recv_buf, loss_acc, loss_in,
     w_sem, in_sem, tgt_sem, sum_send, sum_recv, gat_send, gat_recv, over_send, back_send, take_recv, down_send, out_sem,
-    loss_send, loss_recv, spent_sem, rel_send, rel_over, rel_recv, rel_in, free_sem, table,
+    loss_send, loss_recv, spent_sem, rel_send, rel_over, rel_recv, rel_in, free_sem, table, tile_buf, tile_sem,
 ):
     pos = lax.axis_index("model")
     stage = lax.axis_index("stage")
@@ -105,7 +110,8 @@
 
     def copy_out(kind, chunk):
         src, dst = ((acts.at[0], x_out), (acts.at[1], e_out), (hid.at[0], a_out), (hid.at[1], g_out))[kind]
-        rows = pl.ds(pl.multiple_of(chunk * chunk_rows, chunk_rows), chunk_rows)
+        first = n_grad if kind in (1, 2) else 0
+        rows = pl.ds(pl.multiple_of((chunk - first) * chunk_rows, chunk_rows), chunk_rows)
         return pltpu.make_async_copy(src.at[chunk], dst.at[rows, :], out_sem.at[kind, chunk])
 
     @pl.when(stage == 0)
@@ -273,7 +279,10 @@
                 hid[1, chunk, :, cols] = pre
                 hid[0, chunk, :, cols] = gelu_tanh(pre.astype(F32)).astype(BF16)
             if part == PARTS - 1:
-                copy_out(2, chunk).start()
+
+                @pl.when(chunk >= n_grad)
+                def _():
+                    copy_out(2, chunk).start()
 
                 @pl.when((stage == 0) & (place == 0))
                 def _():
@@ -288,7 +297,10 @@
                 def _():
                     grad_in(chunk).wait()
 
-                copy_out(1, chunk).start()
+                @pl.when(chunk >= n_grad)
+                def _():
+                    copy_out(1, chunk).start()
+
                 copy_out(0, chunk).wait()
             for col in range(part * hid_part, (part + 1) * hid_part, hid_cols):
                 cols = pl.ds(col, hid_cols)
@@ -520,6 +532,29 @@
 
             remote(here, here, gone, rel_in.at[chunk], {"stage": fore_stage}).start()
 
+    tile_rows, tile_cols = tile_buf.shape[1], tile_buf.shape[2]
+    per_row = wts.shape[1] // tile_cols
+    n_tiles = hid_dim // tile_rows * per_row
+    first_tile = (lead[0] + idle[0] + n_grad) * half_pieces
+
+    def copy_tile(index):
+        rows = pl.ds(pl.multiple_of(index // per_row * tile_rows, tile_rows), tile_rows)
+        cols = pl.ds(pl.multiple_of(index % per_row * tile_cols, tile_cols), tile_cols)
+        return pltpu.make_async_copy(tile_buf.at[index % 2], grad_hbm.at[rows, cols], tile_sem.at[index % 2])
+
+    def grad_tile(index):
+        rows = pl.ds(pl.multiple_of(index // per_row * tile_rows, tile_rows), tile_rows)
+        cols = pl.ds(pl.multiple_of(index % per_row * tile_cols, tile_cols), tile_cols)
+
+        @pl.when(index >= 2)
+        def _():
+            copy_tile(index).wait()
+
+        act = hid[0, 0:n_grad, :, rows].reshape(n_grad * chunk_rows, tile_rows)
+        grad = acts[1, 0:n_grad, :, cols].reshape(n_grad * chunk_rows, tile_cols)
+        tile_buf[index % 2] = lax.dot_general(act, grad, (((0,), (0,)), ((), ())), preferred_element_type=F32)
+        copy_tile(index).start()
+
     def loop_step(step, carry):
         for part in range(PARTS):
             first_product(step, part)
@@ -539,9 +574,23 @@
 
         take_step(0, step)
         take_step(1, step)
+        since = step - first_tile
+
+        @pl.when((stage == 0) & (since >= 0) & (since < n_tiles * TILE_STEPS) & (since % TILE_STEPS == 0))
+        def _():
+            grad_tile(since // TILE_STEPS)
+
         return carry
 
     lax.fori_loop(jnp.where(stage == fore_stage, -early, 1 - PARTS), n_steps, loop_step, 0)
+
+    @pl.when(stage > 0)
+    def _():
+        def next_tile(index, carry):
+            grad_tile(index)
+            return carry
+
+        lax.fori_loop(0, n_tiles, next_tile, 0)
 
     for side, owner in ((0, last_pos), (1, 0)):
         owns = (stage == last_stage) & (pos == owner)
@@ -561,12 +610,46 @@
 
     loss_out[...] = jnp.full(loss_out.shape, jnp.sum(loss_in[0] + loss_in[1]) * (0.5 * grad_scale), F32)
 
+    for index in (0, 1):
+        copy_tile(index).wait()
+
     def end_out(chunk, carry):
-        for kind in (1, 2, 3):
-            copy_out(kind, chunk).wait()
+        copy_out(3, chunk).wait()
+
+        @pl.when(chunk >= n_grad)
+        def _():
+            for kind in (1, 2):
+                copy_out(kind, chunk).wait()
+
         return carry
 
     lax.fori_loop(0, n_chunk, end_out, 0)
+
+
+def finish_kernel(first, act, grad, total):
+    total[...] = first[...] + lax.dot_general(act[...], grad[...], (((0,), (0,)), ((), ())), preferred_element_type=F32)
+
+
+def finish_grads(first, act, grad):
+    rows, hid_dim = act.shape
+    model_dim = grad.shape[1]
+    block = min(TILE_ROWS, hid_dim)
+    return pl.pallas_call(
+        finish_kernel,
+        out_shape=jax.ShapeDtypeStruct((hid_dim, model_dim), F32),
+        grid=(hid_dim // block,),
+        in_specs=[
+            pl.BlockSpec((block, model_dim), lambda i: (i, 0)),
+            pl.BlockSpec((rows, block), lambda i: (0, i)),
+            pl.BlockSpec((rows, model_dim), lambda i: (0, 0)),
+        ],
+        out_specs=pl.BlockSpec((block, model_dim), lambda i: (i, 0)),
+        compiler_params=pltpu.CompilerParams(vmem_limit_bytes=51 * 1024 * 1024),
+        cost_estimate=pl.CostEstimate(
+            flops=2 * rows * hid_dim * model_dim, bytes_accessed=8 * hid_dim * model_dim, transcendentals=0
+        ),
+        name="finish_kernel",
+    )(first, act, grad)
 
 
 def solution(mesh):
@@ -585,22 +668,26 @@
         lead = [n_chunk] * (n_stage - 2) + [min(PREV_LEAD, n_chunk), min(LAST_LEAD, n_chunk)]
         idle = [FIRST_IDLE] + [NEXT_IDLE] * (n_stage - 3) + [0, 0]
         n_fore, n_relay = min(FORE_CHUNKS, n_chunk - 1), min(RELAY_CHUNKS, n_chunk - 1)
+        n_grad = min(FIRST_GRADS, n_chunk // 2)
+        rest = rows - n_grad * chunk
+        tile_rows, tile_cols = min(TILE_ROWS, hid_dim), min(TILE_COLS, model_dim)
         kernel = functools.partial(
-            stage_kernel, n_stage, n_model, n_chunk, half_pieces, piece, HOP_LAG, lead, idle, n_fore, n_relay, grad_scale
+            stage_kernel, n_stage, n_model, n_chunk, half_pieces, piece, HOP_LAG, lead, idle, n_fore, n_relay, n_grad, grad_scale
         )
         any_space = pl.BlockSpec(memory_space=pl.ANY)
         dma = pltpu.SemaphoreType.DMA
-        layer_in, layer_grad, layer_act, layer_pre, loss = pl.pallas_call(
+        layer_in, layer_grad, layer_act, layer_pre, first_grads, loss = pl.pallas_call(
             kernel,
             out_shape=(
                 jax.ShapeDtypeStruct((rows, model_dim), BF16),
-                jax.ShapeDtypeStruct((rows, model_dim), BF16),
+                jax.ShapeDtypeStruct((rest, model_dim), BF16),
+                jax.ShapeDtypeStruct((rest, hid_dim), BF16),
                 jax.ShapeDtypeStruct((rows, hid_dim), BF16),
-                jax.ShapeDtypeStruct((rows, hid_dim), BF16),
+                jax.ShapeDtypeStruct((hid_dim, model_dim), F32),
                 jax.ShapeDtypeStruct((8, 128), F32),
             ),
             in_specs=[any_space] * 4,
-            out_specs=(any_space, any_space, any_space, any_space, pl.BlockSpec(memory_space=pltpu.VMEM)),
+            out_specs=(any_space, any_space, any_space, any_space, any_space, pl.BlockSpec(memory_space=pltpu.VMEM)),
             scratch_shapes=[
                 pltpu.VMEM((4, model_dim, hid_dim), BF16),
                 pltpu.VMEM((2, n_chunk, chunk, model_dim), BF16),
@@ -630,6 +717,8 @@
                 dma((n_relay,)),
                 pltpu.SemaphoreType.REGULAR((2,)),
                 pltpu.SMEM((2 * n_chunk + max(idle) + 2 * MARGIN,), jnp.int32),
+                pltpu.VMEM((2, tile_rows, tile_cols), F32),
+                dma((2,)),
             ],
             compiler_params=pltpu.CompilerParams(collective_id=0, has_side_effects=True, vmem_limit_bytes=63 * 1024 * 1024),
             name="stage_kernel",
@@ -644,7 +733,7 @@
             return lax.dot_general(left, right, (((0,), (0,)), ((), ())), preferred_element_type=F32)
 
         grad_in = over_rows(layer_in, layer_pre)
-        grad_out = over_rows(layer_act, layer_grad)
+        grad_out = finish_grads(first_grads, layer_act, layer_grad)
         return grad_in[None, None], grad_out[None, None], loss[0, :1]
 
     return jax.shard_map(

time: 578 us -> 579 us (level)
  Pallas kernels: 539 us -> 560 us
  matrix products: 36.9 us -> 16 us
    dot_general x2 -> x1, matrix products: 36.9 us -> 16 us  [over_rows(): lax.dot_general(left, right, (((0,), (0,)), ((), ())), preferred_element_...]
    pallas_call x0 -> x1, Pallas kernels: none -> 19.8 us  [finish_grads(): pl.pallas_call(finish_kernel, out_shape=jax.ShapeDtypeStruct((hid_dim, mo...]
where the time goes in v9:
time: 579 us; the launch traced here: 578 us
  Pallas kernels  560 us (97%)
  matrix products  16 us (3%)
    pallas_call x1, Pallas kernels, stage_step(): pl.pallas_call(kernel, out_shape=(jax.ShapeDtypeStruct((rows, model_dim),...  540 us
    pallas_call x1, Pallas kernels, finish_grads(): pl.pallas_call(finish_kernel, out_shape=jax.ShapeDtypeStruct((hid_dim, mo...  19.8 us
    dot_general x1, matrix products, over_rows(): lax.dot_general(left, right, (((0,), (0,)), ((), ())), preferred_element_...  16 us

profile of v9, /device:TPU:0, one launch (start us, length us, event | category | flops | bytes accessed | tf_op | source)
XLA Modules:
  0.0 577.6 jit_solution(9040375867397630116)
XLA Ops:
  0.6 539.9 %stage_kernel.1 = (bf16[1536,2048]{1,0:T(8,128)(2,1)}, bf16[768,2048]{1,0:T(8,128)(2,1)}, bf16[768,2048]{1,0:T(8,128)(2,1)}, bf16[1536,2048]{1,0:T(8,128)(2,1)}, f32[2048,2048]{1,0:T(8,128)}, /*index=5*/f32[8,128]{1,0:T(8,128)}) custom-call(bf16[24,64,2048]{2,1,0:T(8,128)(2,1)} %bitcast.13, bf16[24,64,2048]{2,1,0:T(8,128)(2,1)} %bitcast.14, ...), custom_call_target="tpu_custom_call" | custom-call | tf_op jit(solution)/shard_map/stage_kernel/pallas_call | solution.py:679
  540.6 0.0 copy-start
  540.6 0.0 copy-start.1
  540.6 19.8 %finish_kernel.1 = f32[2048,2048]{1,0:T(8,128)} custom-call(f32[2048,2048]{1,0:T(8,128)} %get-tuple-element.11.first, bf16[768,2048]{1,0:T(8,128)(2,1)} %get-tuple-element.12.act, bf16[768,2048]{1,0:T(8,128)(2,1)} %get-tuple-element.13.grad), custom_call_target="tpu_custom_call" | custom-call | flops 6442450944 | bytes 33554432 | tf_op jit(solution)/shard_map/finish_kernel/pallas_call | solution.py:637
  560.4 0.0 copy-done
  560.4 0.0 copy-done.1
  560.4 16.0 %convolution_bitcast_fusion = f32[1,1,2048,2048]{3,2,1,0:T(8,128)} fusion(bf16[1536,2048]{1,0:T(8,128)(2,1)S(1)} %copy-done, bf16[1536,2048]{1,0:T(8,128)(2,1)S(1)} %copy-done.1), kind=kOutput, calls=%fused_computation | convolution fusion | flops 12884901888 | bytes 29360128 | tf_op jit(solution)/shard_map/dot_general | solution.py:733
  576.4 1.2 slice.3
Async XLA Ops:
  540.6 19.8 %copy-start = (bf16[1536,2048]{1,0:T(8,128)(2,1)S(1)}, bf16[1536,2048]{1,0:T(8,128)(2,1)}, u32[]{:S(2)}) copy-start(bf16[1536,2048]{1,0:T(8,128)(2,1)} %get-tuple-element.9) | copy-start | bytes 18874372
  540.6 19.8 %copy-start.1 = (bf16[1536,2048]{1,0:T(8,128)(2,1)S(1)}, bf16[1536,2048]{1,0:T(8,128)(2,1)}, u32[]{:S(2)}) copy-start(bf16[1536,2048]{1,0:T(8,128)(2,1)} %get-tuple-element.10) | copy-start | bytes 18874372

commit v10 on v8

--- a/solution.py
+++ b/solution.py
@@ -24,6 +24,12 @@
 RELAY_CHUNKS = 18
 RELAY_START = 0
 
+FIRST_GRADS = 12
+TILE_ROWS = 256
+TILE_COLS = 1024
+FIRST_TILES = (32, 1)
+NEXT_TILES = (16, 2)
+
 SUM, BACK, GATHER, EARLY, TAKE, FWD, BWD = 256, 512, 1024, 2048, 4096, 8192, 16384
 MARGIN = 8
 
@@ -51,12 +57,12 @@
 
 
 def stage_kernel(
-    n_stage, n_model, n_chunk, half_pieces, piece, hop, lead, idle, n_fore, n_relay, grad_scale,
+    n_stage, n_model, n_chunk, half_pieces, piece, hop, lead, idle, n_fore, n_relay, n_grad, grad_scale,
     inputs_hbm, targets_hbm, w1_hbm, w2_hbm,
-    x_out, e_out, a_out, g_out, loss_out,
+    left_out, right_out, grad_hbm, loss_out,
     wts, acts, hid, send_buf, recv_buf, loss_acc, loss_in,
     w_sem, in_sem, tgt_sem, sum_send, sum_recv, gat_send, gat_recv, over_send, back_send, take_recv, down_send, out_sem,
-    loss_send, loss_recv, spent_sem, rel_send, rel_over, rel_recv, rel_in, free_sem, table,
+    loss_send, loss_recv, spent_sem, rel_send, rel_over, rel_recv, rel_in, free_sem, table, tile_buf, tile_sem, end_buf,
 ):
     pos = lax.axis_index("model")
     stage = lax.axis_index("stage")
@@ -104,8 +110,9 @@
         return pltpu.make_async_copy(targets_hbm.at[:, :, cols], acts.at[1, :, :, cols], tgt_sem)
 
     def copy_out(kind, chunk):
-        src, dst = ((acts.at[0], x_out), (acts.at[1], e_out), (hid.at[0], a_out), (hid.at[1], g_out))[kind]
-        rows = pl.ds(pl.multiple_of(chunk * chunk_rows, chunk_rows), chunk_rows)
+        src = (acts.at[0], hid.at[0], hid.at[1], acts.at[1])[kind]
+        dst = (left_out.at[0], left_out.at[1], right_out.at[0], right_out.at[1])[kind]
+        rows = pl.ds(pl.multiple_of((chunk - n_grad) * chunk_rows, chunk_rows), chunk_rows)
         return pltpu.make_async_copy(src.at[chunk], dst.at[rows, :], out_sem.at[kind, chunk])
 
     @pl.when(stage == 0)
@@ -260,7 +267,10 @@
                 def _():
                     copy_in(chunk).wait()
 
-                copy_out(0, chunk).start()
+                @pl.when(chunk >= n_grad)
+                def _():
+                    copy_out(0, chunk).start()
+
             else:
 
                 @pl.when((stage == 0) & (place == 0))
@@ -273,7 +283,10 @@
                 hid[1, chunk, :, cols] = pre
                 hid[0, chunk, :, cols] = gelu_tanh(pre.astype(F32)).astype(BF16)
             if part == PARTS - 1:
-                copy_out(2, chunk).start()
+
+                @pl.when(chunk >= n_grad)
+                def _():
+                    copy_out(1, chunk).start()
 
                 @pl.when((stage == 0) & (place == 0))
                 def _():
@@ -288,15 +301,20 @@
                 def _():
                     grad_in(chunk).wait()
 
-                copy_out(1, chunk).start()
-                copy_out(0, chunk).wait()
+                @pl.when(chunk >= n_grad)
+                def _():
+                    copy_out(3, chunk).start()
+
             for col in range(part * hid_part, (part + 1) * hid_part, hid_cols):
                 cols = pl.ds(col, hid_cols)
                 grad_act = dot_nn(acts[1, chunk], wts[2, :, cols]).astype(BF16)
                 slope = gelu_slope(hid[1, chunk, :, cols].astype(F32))
                 hid[1, chunk, :, cols] = (slope * grad_act.astype(F32)).astype(BF16)
             if part == PARTS - 1:
-                copy_out(3, chunk).start()
+
+                @pl.when(chunk >= n_grad)
+                def _():
+                    copy_out(2, chunk).start()
 
         if part == 0:
 
@@ -389,9 +407,15 @@
                     def _():
                         send_loss(side)
 
-                @pl.when(jnp.logical_not(scored))
-                def _():
-                    acts[1 - is_back, chunk, :, cols] = whole.astype(BF16)
+                @pl.when(has(word, FWD) & (stage < last_stage))
+                def _():
+                    acts[1, chunk, :, cols] = whole.astype(BF16)
+
+                ended = end_buf.at[side, half_turn, out]
+
+                @pl.when(bwd)
+                def _():
+                    ended[...] = whole.astype(BF16)
 
                 @pl.when(bwd & (index == total - 2 * half_pieces))
                 def _():
@@ -407,12 +431,12 @@
                 @pl.when(bwd & relayed)
                 def _():
                     arrived = rel_recv.at[side, jnp.minimum(index, n_relay * half_pieces - 1)]
-                    remote(acts.at[0, chunk, :, cols], there, gone, arrived, {"stage": 0}).start()
+                    remote(ended, there, gone, arrived, {"stage": 0}).start()
 
                 @pl.when(bwd & jnp.logical_not(relayed))
                 def _():
                     arrived = take_recv.at[side, index]
-                    remote(acts.at[0, chunk, :, cols], there, gone, arrived, {"stage": stage - 1}).start()
+                    remote(ended, there, gone, arrived, {"stage": stage - 1}).start()
 
     def gather_step(side, step):
         rank = rank_of(side)
@@ -520,6 +544,37 @@
 
             remote(here, here, gone, rel_in.at[chunk], {"stage": fore_stage}).start()
 
+    tile_rows, tile_cols = tile_buf.shape[1], tile_buf.shape[2]
+    per_row = wts.shape[1] // tile_cols
+    n_tiles = hid_dim // tile_rows * per_row
+
+    def copy_tile(which, index):
+        rows = pl.ds(pl.multiple_of(index // per_row * tile_rows, tile_rows), tile_rows)
+        cols = pl.ds(pl.multiple_of(index % per_row * tile_cols, tile_cols), tile_cols)
+        return pltpu.make_async_copy(tile_buf.at[index % 2], grad_hbm.at[which, rows, cols], tile_sem.at[index % 2])
+
+    def grad_tile(number):
+        for which, index in ((1, number), (0, number - n_tiles)):
+
+            @pl.when((index >= 0) & (index < n_tiles))
+            def _():
+                rows = pl.ds(pl.multiple_of(index // per_row * tile_rows, tile_rows), tile_rows)
+                cols = pl.ds(pl.multiple_of(index % per_row * tile_cols, tile_cols), tile_cols)
+
+                @pl.when(number >= 2)
+                def _():
+                    copy_tile(which, index).wait()
+
+                inputs, grads = (acts.at[0], hid.at[1]) if which == 0 else (hid.at[0], acts.at[1])
+                lefts = inputs[0:n_grad, :, rows].reshape(n_grad * chunk_rows, tile_rows)
+                rights = grads[0:n_grad, :, cols].reshape(n_grad * chunk_rows, tile_cols)
+                tile_buf[index % 2] = lax.dot_general(lefts, rights, (((0,), (0,)), ((), ())), preferred_element_type=F32)
+                copy_tile(which, index).start()
+
+    in_loop = jnp.where(stage == 0, FIRST_TILES[0], jnp.where(stage == 1, NEXT_TILES[0], 0))
+    pitch = jnp.where(stage == 0, FIRST_TILES[1], NEXT_TILES[1])
+    first_tile = (n_first + n_grad) * half_pieces
+
     def loop_step(step, carry):
         for part in range(PARTS):
             first_product(step, part)
@@ -539,9 +594,21 @@
 
         take_step(0, step)
         take_step(1, step)
+        since = step - first_tile
+
+        @pl.when((since >= 0) & (since < in_loop * pitch) & (since % pitch == 0))
+        def _():
+            grad_tile(since // pitch)
+
         return carry
 
     lax.fori_loop(jnp.where(stage == fore_stage, -early, 1 - PARTS), n_steps, loop_step, 0)
+
+    def next_tile(number, carry):
+        grad_tile(number)
+        return carry
+
+    lax.fori_loop(in_loop, 2 * n_tiles, next_tile, 0)
 
     for side, owner in ((0, last_pos), (1, 0)):
         owns = (stage == last_stage) & (pos == owner)
@@ -561,12 +628,52 @@
 
     loss_out[...] = jnp.full(loss_out.shape, jnp.sum(loss_in[0] + loss_in[1]) * (0.5 * grad_scale), F32)
 
+    for index in (0, 1):
+        copy_tile(0, index).wait()
+
     def end_out(chunk, carry):
-        for kind in (1, 2, 3):
+        for kind in range(4):
             copy_out(kind, chunk).wait()
         return carry
 
-    lax.fori_loop(0, n_chunk, end_out, 0)
+    lax.fori_loop(n_grad, n_chunk, end_out, 0)
+
+
+def finish_kernel(first, lefts, rights, grad_in, grad_out):
+    def whole():
+        return first[0] + lax.dot_general(lefts[0], rights[0], (((0,), (0,)), ((), ())), preferred_element_type=F32)
+
+    @pl.when(pl.program_id(0) == 0)
+    def _():
+        grad_in[...] = whole()
+
+    @pl.when(pl.program_id(0) == 1)
+    def _():
+        grad_out[...] = whole()
+
+
+def finish_grads(first, lefts, rights):
+    rows, dim = lefts.shape[1:]
+    block = min(TILE_ROWS, dim)
+    blocks = dim // block
+    shape = jax.ShapeDtypeStruct((dim, dim), F32)
+    return pl.pallas_call(
+        finish_kernel,
+        out_shape=(shape, shape),
+        grid=(2, blocks),
+        in_specs=[
+            pl.BlockSpec((1, block, dim), lambda which, i: (which, i, 0)),
+            pl.BlockSpec((1, rows, block), lambda which, i: (which, 0, i)),
+            pl.BlockSpec((1, rows, dim), lambda which, i: (which, 0, 0)),
+        ],
+        out_specs=(
+            pl.BlockSpec((block, dim), lambda which, i: (i * (1 - which) + (blocks - 1) * which, 0)),
+            pl.BlockSpec((block, dim), lambda which, i: (i * which, 0)),
+        ),
+        compiler_params=pltpu.CompilerParams(vmem_limit_bytes=60 * 1024 * 1024),
+        cost_estimate=pl.CostEstimate(flops=4 * rows * dim * dim, bytes_accessed=16 * dim * dim, transcendentals=0),
+        name="finish_kernel",
+    )(first, lefts, rights)
 
 
 def solution(mesh):
@@ -585,22 +692,24 @@
         lead = [n_chunk] * (n_stage - 2) + [min(PREV_LEAD, n_chunk), min(LAST_LEAD, n_chunk)]
         idle = [FIRST_IDLE] + [NEXT_IDLE] * (n_stage - 3) + [0, 0]
         n_fore, n_relay = min(FORE_CHUNKS, n_chunk - 1), min(RELAY_CHUNKS, n_chunk - 1)
+        n_grad = min(FIRST_GRADS, n_chunk // 2)
+        rest = rows - n_grad * chunk
+        tile_rows, tile_cols = min(TILE_ROWS, hid_dim), min(TILE_COLS, model_dim)
         kernel = functools.partial(
-            stage_kernel, n_stage, n_model, n_chunk, half_pieces, piece, HOP_LAG, lead, idle, n_fore, n_relay, grad_scale
+            stage_kernel, n_stage, n_model, n_chunk, half_pieces, piece, HOP_LAG, lead, idle, n_fore, n_relay, n_grad, grad_scale
         )
         any_space = pl.BlockSpec(memory_space=pl.ANY)
         dma = pltpu.SemaphoreType.DMA
-        layer_in, layer_grad, layer_act, layer_pre, loss = pl.pallas_call(
+        lefts, rights, first_grads, loss = pl.pallas_call(
             kernel,
             out_shape=(
-                jax.ShapeDtypeStruct((rows, model_dim), BF16),
-                jax.ShapeDtypeStruct((rows, model_dim), BF16),
-                jax.ShapeDtypeStruct((rows, hid_dim), BF16),
-                jax.ShapeDtypeStruct((rows, hid_dim), BF16),
+                jax.ShapeDtypeStruct((2, rest, model_dim), BF16),
+                jax.ShapeDtypeStruct((2, rest, model_dim), BF16),
+                jax.ShapeDtypeStruct((2, hid_dim, model_dim), F32),
                 jax.ShapeDtypeStruct((8, 128), F32),
             ),
             in_specs=[any_space] * 4,
-            out_specs=(any_space, any_space, any_space, any_space, pl.BlockSpec(memory_space=pltpu.VMEM)),
+            out_specs=(any_space, any_space, any_space, pl.BlockSpec(memory_space=pltpu.VMEM)),
             scratch_shapes=[
                 pltpu.VMEM((4, model_dim, hid_dim), BF16),
                 pltpu.VMEM((2, n_chunk, chunk, model_dim), BF16),
@@ -630,6 +739,9 @@
                 dma((n_relay,)),
                 pltpu.SemaphoreType.REGULAR((2,)),
                 pltpu.SMEM((2 * n_chunk + max(idle) + 2 * MARGIN,), jnp.int32),
+                pltpu.VMEM((2, tile_rows, tile_cols), F32),
+                dma((2,)),
+                pltpu.VMEM((2, 2, half_pieces, chunk, piece), BF16),
             ],
             compiler_params=pltpu.CompilerParams(collective_id=0, has_side_effects=True, vmem_limit_bytes=63 * 1024 * 1024),
             name="stage_kernel",
@@ -640,11 +752,7 @@
             w_out.reshape(hid_dim, model_dim),
         )
 
-        def over_rows(left, right):
-            return lax.dot_general(left, right, (((0,), (0,)), ((), ())), preferred_element_type=F32)
-
-        grad_in = over_rows(layer_in, layer_pre)
-        grad_out = over_rows(layer_act, layer_grad)
+        grad_in, grad_out = finish_grads(first_grads, lefts, rights)
         return grad_in[None, None], grad_out[None, None], loss[0, :1]
 
     return jax.shard_map(

time: 578 us -> 582 us (level)
  Pallas kernels: 539 us -> 580 us
  matrix products: 36.9 us -> 0 us
    pallas_call x1 -> x2, Pallas kernels: 539 us -> 580 us  [the longest x1 543 us: stage_step(): pl.pallas_call(kernel, out_shape=(jax.ShapeDtypeStruct((2, rest, model_di...]
    dot_general x2 -> x0, matrix products: 36.9 us -> none  [over_rows(): lax.dot_general(left, right, (((0,), (0,)), ((), ())), preferred_element_...]
where the time goes in v10:
time: 582 us
  Pallas kernels  580 us (100%)
    pallas_call x1, Pallas kernels, stage_step(): pl.pallas_call(kernel, out_shape=(jax.ShapeDtypeStruct((2, rest, model_di...  543 us
    pallas_call x1, Pallas kernels, finish_grads(): pl.pallas_call(finish_kernel, out_shape=(shape, shape), grid=(2, blocks),...  36.8 us

profile of v10, /device:TPU:0, one launch (start us, length us, event | category | flops | bytes accessed | tf_op | source)
XLA Modules:
  0.0 581.5 jit_solution(8395911229279819464)
XLA Ops:
  0.6 542.9 %stage_kernel.1 = (bf16[2,768,2048]{2,1,0:T(8,128)(2,1)}, bf16[2,768,2048]{2,1,0:T(8,128)(2,1)}, f32[2,2048,2048]{2,1,0:T(8,128)}, f32[8,128]{1,0:T(8,128)}) custom-call(bf16[24,64,2048]{2,1,0:T(8,128)(2,1)} %bitcast.9, bf16[24,64,2048]{2,1,0:T(8,128)(2,1)} %bitcast.10, bf16[2048,2048]{1,0:T(8,128)(2,1)} %bitcast.7, bf16[2048,2048]{1,0:T(8,128)(2,1)} %bitcast.8), custom_call_target="tpu_custom_call" | custom-call | tf_op jit(solution)/shard_map/stage_kernel/pallas_call | solution.py:703
  543.5 1.2 slice.3
  544.7 36.8 %finish_kernel.1 = (f32[2048,2048]{1,0:T(8,128)}, f32[2048,2048]{1,0:T(8,128)}) custom-call(f32[2,2048,2048]{2,1,0:T(8,128)} %get-tuple-element.9.first, bf16[2,768,2048]{2,1,0:T(8,128)(2,1)} %get-tuple-element.10.lefts, bf16[2,768,2048]{2,1,0:T(8,128)(2,1)} %get-tuple-element.11.rights), custom_call_target="tpu_custom_call" | custom-call | flops 12884901888 | bytes 67108864 | tf_op jit(solution)/shard_map/finish_kernel/pallas_call | solution.py:660

commit v11 on v10

--- a/solution.py
+++ b/solution.py
@@ -24,9 +24,10 @@
 RELAY_CHUNKS = 18
 RELAY_START = 0
 
-FIRST_GRADS = 12
+FIRST_GRADS = 14
 TILE_ROWS = 256
 TILE_COLS = 1024
+IN_FLIGHT = 5
 FIRST_TILES = (32, 1)
 NEXT_TILES = (16, 2)
 
@@ -639,17 +640,75 @@
     lax.fori_loop(n_grad, n_chunk, end_out, 0)
 
 
-def finish_kernel(first, lefts, rights, grad_in, grad_out):
-    def whole():
-        return first[0] + lax.dot_general(lefts[0], rights[0], (((0,), (0,)), ((), ())), preferred_element_type=F32)
-
-    @pl.when(pl.program_id(0) == 0)
-    def _():
-        grad_in[...] = whole()
-
-    @pl.when(pl.program_id(0) == 1)
-    def _():
-        grad_out[...] = whole()
+def finish_kernel(first_hbm, lefts_hbm, rights_hbm, grad_in, grad_out, sums, lefts, rights, sum_in, sum_out, operand_in):
+    block = sums.shape[1]
+    blocks = grad_in.shape[0] // block
+    half = lefts.shape[1] // 2
+
+    def copy_operands(which):
+        pairs = ((rights_hbm, rights, 0), (lefts_hbm, lefts, 1))
+        return [
+            pltpu.make_async_copy(
+                src.at[which, pl.ds(part * half, half), :], dst.at[which, pl.ds(part * half, half), :], operand_in.at[which, kind, part]
+            )
+            for src, dst, kind in pairs
+            for part in (0, 1)
+        ]
+
+    def rows_of(number):
+        return pl.ds(pl.multiple_of(number % blocks * block, block), block)
+
+    def copy_first(number):
+        return pltpu.make_async_copy(first_hbm.at[number // blocks, rows_of(number), :], sums.at[number], sum_in.at[number])
+
+    def copy_result(number, which):
+        return pltpu.make_async_copy(sums.at[number], (grad_in, grad_out)[which].at[rows_of(number), :], sum_out.at[number])
+
+    for copy in copy_operands(0):
+        copy.start()
+    for number in range(IN_FLIGHT):
+        copy_first(number).start()
+
+    def one(number, carry):
+        for which in (0, 1):
+
+            @pl.when(number == which * blocks)
+            def _():
+                for copy in copy_operands(which):
+                    copy.wait()
+
+        @pl.when(number == 1)
+        def _():
+            for copy in copy_operands(1):
+                copy.start()
+
+        copy_first(number).wait()
+
+        @pl.when(number + IN_FLIGHT < 2 * blocks)
+        def _():
+            copy_first(number + IN_FLIGHT).start()
+
+        which = number // blocks
+        part = lax.dot_general(
+            lefts[which, :, rows_of(number)], rights[which], (((0,), (0,)), ((), ())), preferred_element_type=F32
+        )
+        sums[number] = sums[number] + part
+
+        for kind in (0, 1):
+
+            @pl.when(which == kind)
+            def _():
+                copy_result(number, kind).start()
+
+        return carry
+
+    lax.fori_loop(0, 2 * blocks, one, 0)
+
+    def end(number, carry):
+        copy_result(number, 0).wait()
+        return carry
+
+    lax.fori_loop(0, 2 * blocks, end, 0)
 
 
 def finish_grads(first, lefts, rights):
@@ -657,20 +716,22 @@
     block = min(TILE_ROWS, dim)
     blocks = dim // block
     shape = jax.ShapeDtypeStruct((dim, dim), F32)
+    any_space = pl.BlockSpec(memory_space=pl.ANY)
+    dma = pltpu.SemaphoreType.DMA
     return pl.pallas_call(
         finish_kernel,
         out_shape=(shape, shape),
-        grid=(2, blocks),
-        in_specs=[
-            pl.BlockSpec((1, block, dim), lambda which, i: (which, i, 0)),
-            pl.BlockSpec((1, rows, block), lambda which, i: (which, 0, i)),
-            pl.BlockSpec((1, rows, dim), lambda which, i: (which, 0, 0)),
+        in_specs=[any_space] * 3,
+        out_specs=(any_space, any_space),
+        scratch_shapes=[
+            pltpu.VMEM((2 * blocks, block, dim), F32),
+            pltpu.VMEM((2, rows, dim), BF16),
+            pltpu.VMEM((2, rows, dim), BF16),
+            dma((2 * blocks,)),
+            dma((2 * blocks,)),
+            dma((2, 2, 2)),
         ],
-        out_specs=(
-            pl.BlockSpec((block, dim), lambda which, i: (i * (1 - which) + (blocks - 1) * which, 0)),
-            pl.BlockSpec((block, dim), lambda which, i: (i * which, 0)),
-        ),
-        compiler_params=pltpu.CompilerParams(vmem_limit_bytes=60 * 1024 * 1024),
+        compiler_params=pltpu.CompilerParams(vmem_limit_bytes=62 * 1024 * 1024),
         cost_estimate=pl.CostEstimate(flops=4 * rows * dim * dim, bytes_accessed=16 * dim * dim, transcendentals=0),
         name="finish_kernel",
     )(first, lefts, rights)

time: 582 us -> 572 us (0.983)
  Pallas kernels: 580 us -> 570 us
    pallas_call x1, Pallas kernels: 36.8 us -> 27.4 us  [finish_grads(): pl.pallas_call(finish_kernel, out_shape=(shape, shape), in_specs=[any_spa...]
where the time goes in v11:
time: 572 us
  Pallas kernels  570 us (100%)
    pallas_call x1, Pallas kernels, stage_step(): pl.pallas_call(kernel, out_shape=(jax.ShapeDtypeStruct((2, rest, model_di...  543 us
    pallas_call x1, Pallas kernels, finish_grads(): pl.pallas_call(finish_kernel, out_shape=(shape, shape), in_specs=[any_spa...  27.4 us

profile of v11, /device:TPU:0, one launch (start us, length us, event | category | flops | bytes accessed | tf_op | source)
XLA Modules:
  0.0 572.0 jit_solution(10918083023032140351)
XLA Ops:
  0.6 542.8 %stage_kernel.1 = (bf16[2,768,2048]{2,1,0:T(8,128)(2,1)}, bf16[2,768,2048]{2,1,0:T(8,128)(2,1)}, f32[2,2048,2048]{2,1,0:T(8,128)}, f32[8,128]{1,0:T(8,128)}) custom-call(bf16[24,64,2048]{2,1,0:T(8,128)(2,1)} %bitcast.9, bf16[24,64,2048]{2,1,0:T(8,128)(2,1)} %bitcast.10, bf16[2048,2048]{1,0:T(8,128)(2,1)} %bitcast.7, bf16[2048,2048]{1,0:T(8,128)(2,1)} %bitcast.8), custom_call_target="tpu_custom_call" | custom-call | tf_op jit(solution)/shard_map/stage_kernel/pallas_call | solution.py:764
  543.4 1.2 slice.3
  544.6 27.4 %finish_kernel.1 = (f32[2048,2048]{1,0:T(8,128)}, f32[2048,2048]{1,0:T(8,128)}) custom-call(f32[2,2048,2048]{2,1,0:T(8,128)} %get-tuple-element.9.first_hbm, bf16[2,768,2048]{2,1,0:T(8,128)(2,1)} %get-tuple-element.10.lefts_hbm, bf16[2,768,2048]{2,1,0:T(8,128)(2,1)} %get-tuple-element.11.rights_hbm), custom_call_target="tpu_custom_call" | custom-call | flops 12884901888 | bytes 67108864 | tf_op jit(solution)/shard_map/finish_kernel/pallas_call | solution.py:721

commit v12 on v11

--- a/solution.py
+++ b/solution.py
@@ -24,12 +24,12 @@
 RELAY_CHUNKS = 18
 RELAY_START = 0
 
-FIRST_GRADS = 14
+FIRST_GRADS = 12
 TILE_ROWS = 256
 TILE_COLS = 1024
-IN_FLIGHT = 5
+IN_FLIGHT = 8
 FIRST_TILES = (32, 1)
-NEXT_TILES = (16, 2)
+NEXT_TILES = (16, 3)
 
 SUM, BACK, GATHER, EARLY, TAKE, FWD, BWD = 256, 512, 1024, 2048, 4096, 8192, 16384
 MARGIN = 8
@@ -640,7 +640,9 @@
     lax.fori_loop(n_grad, n_chunk, end_out, 0)
 
 
-def finish_kernel(first_hbm, lefts_hbm, rights_hbm, grad_in, grad_out, sums, lefts, rights, sum_in, sum_out, operand_in):
+def finish_kernel(
+    first_hbm, lefts_hbm, rights_hbm, loss_hbm, grad_in, grad_out, loss_out, sums, lefts, rights, loss, sum_in, sum_out, operand_in, loss_sem
+):
     block = sums.shape[1]
     blocks = grad_in.shape[0] // block
     half = lefts.shape[1] // 2
@@ -664,10 +666,12 @@
     def copy_result(number, which):
         return pltpu.make_async_copy(sums.at[number], (grad_in, grad_out)[which].at[rows_of(number), :], sum_out.at[number])
 
+    copy_loss = pltpu.make_async_copy(loss_hbm, loss, loss_sem)
     for copy in copy_operands(0):
         copy.start()
     for number in range(IN_FLIGHT):
         copy_first(number).start()
+    copy_loss.start()
 
     def one(number, carry):
         for which in (0, 1):
@@ -703,6 +707,8 @@
         return carry
 
     lax.fori_loop(0, 2 * blocks, one, 0)
+    copy_loss.wait()
+    loss_out[0] = loss[0, 0]
 
     def end(number, carry):
         copy_result(number, 0).wait()
@@ -711,7 +717,7 @@
     lax.fori_loop(0, 2 * blocks, end, 0)
 
 
-def finish_grads(first, lefts, rights):
+def finish_grads(first, lefts, rights, loss):
     rows, dim = lefts.shape[1:]
     block = min(TILE_ROWS, dim)
     blocks = dim // block
@@ -720,21 +726,23 @@
     dma = pltpu.SemaphoreType.DMA
     return pl.pallas_call(
         finish_kernel,
-        out_shape=(shape, shape),
-        in_specs=[any_space] * 3,
-        out_specs=(any_space, any_space),
+        out_shape=(shape, shape, jax.ShapeDtypeStruct((1,), F32)),
+        in_specs=[any_space] * 4,
+        out_specs=(any_space, any_space, pl.BlockSpec(memory_space=pltpu.SMEM)),
         scratch_shapes=[
             pltpu.VMEM((2 * blocks, block, dim), F32),
             pltpu.VMEM((2, rows, dim), BF16),
             pltpu.VMEM((2, rows, dim), BF16),
+            pltpu.VMEM(loss.shape, F32),
             dma((2 * blocks,)),
             dma((2 * blocks,)),
             dma((2, 2, 2)),
+            dma,
         ],
         compiler_params=pltpu.CompilerParams(vmem_limit_bytes=62 * 1024 * 1024),
         cost_estimate=pl.CostEstimate(flops=4 * rows * dim * dim, bytes_accessed=16 * dim * dim, transcendentals=0),
         name="finish_kernel",
-    )(first, lefts, rights)
+    )(first, lefts, rights, loss)
 
 
 def solution(mesh):
@@ -813,8 +821,8 @@
             w_out.reshape(hid_dim, model_dim),
         )
 
-        grad_in, grad_out = finish_grads(first_grads, lefts, rights)
-        return grad_in[None, None], grad_out[None, None], loss[0, :1]
+        grad_in, grad_out, loss = finish_grads(first_grads, lefts, rights, loss)
+        return grad_in[None, None], grad_out[None, None], loss
 
     return jax.shard_map(
         stage_step,

time: 572 us -> 571 us (level)
  no operation moved by 1% of the time
where the time goes in v12:
time: 571 us
  Pallas kernels  570 us (100%)
    pallas_call x1, Pallas kernels, stage_step(): pl.pallas_call(kernel, out_shape=(jax.ShapeDtypeStruct((2, rest, model_di...  542 us
    pallas_call x1, Pallas kernels, finish_grads(): pl.pallas_call(finish_kernel, out_shape=(shape, shape, jax.ShapeDtypeStru...  28.2 us

profile of v12, /device:TPU:0, one launch (start us, length us, event | category | flops | bytes accessed | tf_op | source)
XLA Modules:
  0.0 571.0 jit_solution(10016450405707004594)
XLA Ops:
  0.6 542.2 %stage_kernel.1 = (bf16[2,768,2048]{2,1,0:T(8,128)(2,1)}, bf16[2,768,2048]{2,1,0:T(8,128)(2,1)}, f32[2,2048,2048]{2,1,0:T(8,128)}, f32[8,128]{1,0:T(8,128)}) custom-call(bf16[24,64,2048]{2,1,0:T(8,128)(2,1)} %bitcast.8, bf16[24,64,2048]{2,1,0:T(8,128)(2,1)} %bitcast.9, bf16[2048,2048]{1,0:T(8,128)(2,1)} %bitcast.6, bf16[2048,2048]{1,0:T(8,128)(2,1)} %bitcast.7), custom_call_target="tpu_custom_call" | custom-call | tf_op jit(solution)/shard_map/stage_kernel/pallas_call | solution.py:772
  542.8 28.2 %finish_kernel.1 = (f32[2048,2048]{1,0:T(8,128)}, f32[2048,2048]{1,0:T(8,128)}, f32[1]{0:T(128)}) custom-call(f32[2,2048,2048]{2,1,0:T(8,128)} %get-tuple-element.10.first_hbm, bf16[2,768,2048]{2,1,0:T(8,128)(2,1)} %get-tuple-element.11.lefts_hbm, bf16[2,768,2048]{2,1,0:T(8,128)(2,1)} %get-tuple-element.12.rights_hbm, f32[8,128]{1,0:T(8,128)} %get-tuple-element.13.loss_hbm), custom_call_target="tpu_custom_call" | custom-call | flops 12884901888 | bytes 67108864 | tf_op jit(solution)/shard_map/finish_kernel/pallas_call | solution.py:727

commit v13 on v12

--- a/solution.py
+++ b/solution.py
@@ -27,9 +27,10 @@
 FIRST_GRADS = 12
 TILE_ROWS = 256
 TILE_COLS = 1024
-IN_FLIGHT = 8
+IN_FLIGHT = 6
+AT_START = 2
 FIRST_TILES = (32, 1)
-NEXT_TILES = (16, 3)
+NEXT_TILES = (24, 2)
 
 SUM, BACK, GATHER, EARLY, TAKE, FWD, BWD = 256, 512, 1024, 2048, 4096, 8192, 16384
 MARGIN = 8
@@ -669,7 +670,7 @@
     copy_loss = pltpu.make_async_copy(loss_hbm, loss, loss_sem)
     for copy in copy_operands(0):
         copy.start()
-    for number in range(IN_FLIGHT):
+    for number in range(AT_START):
         copy_first(number).start()
     copy_loss.start()
 
@@ -681,12 +682,17 @@
                 for copy in copy_operands(which):
                     copy.wait()
 
-        @pl.when(number == 1)
+        copy_first(number).wait()
+
+        @pl.when(number == 0)
+        def _():
+            for ahead in range(AT_START, IN_FLIGHT):
+                copy_first(ahead).start()
+
+        @pl.when(number == 2)
         def _():
             for copy in copy_operands(1):
                 copy.start()
-
-        copy_first(number).wait()
 
         @pl.when(number + IN_FLIGHT < 2 * blocks)
         def _():

time: 571 us -> 572 us (level)
  no operation moved by 1% of the time
where the time goes in v13:
time: 572 us
  Pallas kernels  571 us (100%)
    pallas_call x1, Pallas kernels, stage_step(): pl.pallas_call(kernel, out_shape=(jax.ShapeDtypeStruct((2, rest, model_di...  543 us
    pallas_call x1, Pallas kernels, finish_grads(): pl.pallas_call(finish_kernel, out_shape=(shape, shape, jax.ShapeDtypeStru...  28.2 us

profile of v13, /device:TPU:0, one launch (start us, length us, event | category | flops | bytes accessed | tf_op | source)
XLA Modules:
  0.0 571.8 jit_solution(14506785456217588649)
XLA Ops:
  0.6 543.0 %stage_kernel.1 = (bf16[2,768,2048]{2,1,0:T(8,128)(2,1)}, bf16[2,768,2048]{2,1,0:T(8,128)(2,1)}, f32[2,2048,2048]{2,1,0:T(8,128)}, f32[8,128]{1,0:T(8,128)}) custom-call(bf16[24,64,2048]{2,1,0:T(8,128)(2,1)} %bitcast.8, bf16[24,64,2048]{2,1,0:T(8,128)(2,1)} %bitcast.9, bf16[2048,2048]{1,0:T(8,128)(2,1)} %bitcast.6, bf16[2048,2048]{1,0:T(8,128)(2,1)} %bitcast.7), custom_call_target="tpu_custom_call" | custom-call | tf_op jit(solution)/shard_map/stage_kernel/pallas_call | solution.py:778
  543.6 28.2 %finish_kernel.1 = (f32[2048,2048]{1,0:T(8,128)}, f32[2048,2048]{1,0:T(8,128)}, f32[1]{0:T(128)}) custom-call(f32[2,2048,2048]{2,1,0:T(8,128)} %get-tuple-element.10.first_hbm, bf16[2,768,2048]{2,1,0:T(8,128)(2,1)} %get-tuple-element.11.lefts_hbm, bf16[2,768,2048]{2,1,0:T(8,128)(2,1)} %get-tuple-element.12.rights_hbm, f32[8,128]{1,0:T(8,128)} %get-tuple-element.13.loss_hbm), custom_call_target="tpu_custom_call" | custom-call | flops 12884901888 | bytes 67108864 | tf_op jit(solution)/shard_map/finish_kernel/pallas_call | solution.py:733

commit v14 on v12

--- a/solution.py
+++ b/solution.py
@@ -17,11 +17,11 @@
 HOP_LAG = 2
 RECV_SLOTS = 8
 LAST_LEAD = 5
-PREV_LEAD = 16
+PREV_LEAD = 15
 FIRST_IDLE = 12
 NEXT_IDLE = 7
-FORE_CHUNKS = 6
-RELAY_CHUNKS = 18
+FORE_CHUNKS = 7
+RELAY_CHUNKS = 19
 RELAY_START = 0
 
 FIRST_GRADS = 12

time: 571 us -> 571 us (level)
  no operation moved by 1% of the time
where the time goes in v14:
time: 571 us
  Pallas kernels  571 us (100%)
    pallas_call x1, Pallas kernels, stage_step(): pl.pallas_call(kernel, out_shape=(jax.ShapeDtypeStruct((2, rest, model_di...  542 us
    pallas_call x1, Pallas kernels, finish_grads(): pl.pallas_call(finish_kernel, out_shape=(shape, shape, jax.ShapeDtypeStru...  28.4 us

profile of v14, /device:TPU:0, one launch (start us, length us, event | category | flops | bytes accessed | tf_op | source)
XLA Modules:
  0.0 571.2 jit_solution(11230619984738038648)
XLA Ops:
  0.6 542.1 %stage_kernel.1 = (bf16[2,768,2048]{2,1,0:T(8,128)(2,1)}, bf16[2,768,2048]{2,1,0:T(8,128)(2,1)}, f32[2,2048,2048]{2,1,0:T(8,128)}, f32[8,128]{1,0:T(8,128)}) custom-call(bf16[24,64,2048]{2,1,0:T(8,128)(2,1)} %bitcast.8, bf16[24,64,2048]{2,1,0:T(8,128)(2,1)} %bitcast.9, bf16[2048,2048]{1,0:T(8,128)(2,1)} %bitcast.6, bf16[2048,2048]{1,0:T(8,128)(2,1)} %bitcast.7), custom_call_target="tpu_custom_call" | custom-call | tf_op jit(solution)/shard_map/stage_kernel/pallas_call | solution.py:772
  542.7 28.4 %finish_kernel.1 = (f32[2048,2048]{1,0:T(8,128)}, f32[2048,2048]{1,0:T(8,128)}, f32[1]{0:T(128)}) custom-call(f32[2,2048,2048]{2,1,0:T(8,128)} %get-tuple-element.10.first_hbm, bf16[2,768,2048]{2,1,0:T(8,128)(2,1)} %get-tuple-element.11.lefts_hbm, bf16[2,768,2048]{2,1,0:T(8,128)(2,1)} %get-tuple-element.12.rights_hbm, f32[8,128]{1,0:T(8,128)} %get-tuple-element.13.loss_hbm), custom_call_target="tpu_custom_call" | custom-call | flops 12884901888 | bytes 67108864 | tf_op jit(solution)/shard_map/finish_kernel/pallas_call | solution.py:727

commit v15 on v14

--- a/solution.py
+++ b/solution.py
@@ -24,12 +24,12 @@
 RELAY_CHUNKS = 19
 RELAY_START = 0
 
-FIRST_GRADS = 12
+FIRST_GRADS = 14
 TILE_ROWS = 256
 TILE_COLS = 1024
 IN_FLIGHT = 8
 FIRST_TILES = (32, 1)
-NEXT_TILES = (16, 3)
+NEXT_TILES = (14, 2)
 
 SUM, BACK, GATHER, EARLY, TAKE, FWD, BWD = 256, 512, 1024, 2048, 4096, 8192, 16384
 MARGIN = 8

time: 571 us -> 572 us (level)
  no operation moved by 1% of the time
where the time goes in v15:
time: 572 us
  Pallas kernels  571 us (100%)
    pallas_call x1, Pallas kernels, stage_step(): pl.pallas_call(kernel, out_shape=(jax.ShapeDtypeStruct((2, rest, model_di...  542 us
    pallas_call x1, Pallas kernels, finish_grads(): pl.pallas_call(finish_kernel, out_shape=(shape, shape, jax.ShapeDtypeStru...  28.4 us

profile of v15, /device:TPU:0, one launch (start us, length us, event | category | flops | bytes accessed | tf_op | source)
XLA Modules:
  0.0 571.5 jit_solution(17869344325510212720)
XLA Ops:
  0.6 542.4 %stage_kernel.1 = (bf16[2,768,2048]{2,1,0:T(8,128)(2,1)}, bf16[2,768,2048]{2,1,0:T(8,128)(2,1)}, f32[2,2048,2048]{2,1,0:T(8,128)}, f32[8,128]{1,0:T(8,128)}) custom-call(bf16[24,64,2048]{2,1,0:T(8,128)(2,1)} %bitcast.8, bf16[24,64,2048]{2,1,0:T(8,128)(2,1)} %bitcast.9, bf16[2048,2048]{1,0:T(8,128)(2,1)} %bitcast.6, bf16[2048,2048]{1,0:T(8,128)(2,1)} %bitcast.7), custom_call_target="tpu_custom_call" | custom-call | tf_op jit(solution)/shard_map/stage_kernel/pallas_call | solution.py:772
  543.1 28.4 %finish_kernel.1 = (f32[2048,2048]{1,0:T(8,128)}, f32[2048,2048]{1,0:T(8,128)}, f32[1]{0:T(128)}) custom-call(f32[2,2048,2048]{2,1,0:T(8,128)} %get-tuple-element.10.first_hbm, bf16[2,768,2048]{2,1,0:T(8,128)(2,1)} %get-tuple-element.11.lefts_hbm, bf16[2,768,2048]{2,1,0:T(8,128)(2,1)} %get-tuple-element.12.rights_hbm, f32[8,128]{1,0:T(8,128)} %get-tuple-element.13.loss_hbm), custom_call_target="tpu_custom_call" | custom-call | flops 12884901888 | bytes 67108864 | tf_op jit(solution)/shard_map/finish_kernel/pallas_call | solution.py:727
